TPU v7x, 32 devices: a whole 2x2x4 slice. The times are simulated.
32 devices in a mesh: dp: 4 (over y, core), row: 4 (over z), col: 2 (over x).
Axes of the slice: x: 2, y: 2, z: 4, core: 2. Of those that a mesh axis runs over, the one named last changes fastest.
Arguments:
- tokens: bfloat16 [8192, 2048], P(('dp', 'col'), 'row'), may hold values from -6 to 6
- gain_attn: bfloat16 [2048], P('row'), may hold values from 0.5 to 1.5
- w_query: bfloat16 [2048, 2048], P('row', 'col'), may hold values from -0.125 to 0.125
- w_key: bfloat16 [2048, 256], P('row', 'col'), may hold values from -0.125 to 0.125
- w_value: bfloat16 [2048, 256], P('row', 'col'), may hold values from -0.125 to 0.125
- w_out: bfloat16 [2048, 2048], P('col', 'row'), may hold values from -0.5 to 0.5
- gain_mlp: bfloat16 [2048], P('row'), may hold values from 0.5 to 1.5
- w_gate: bfloat16 [2048, 5632], P('row', 'col'), may hold values from -0.125 to 0.125
- w_up: bfloat16 [2048, 5632], P('row', 'col'), may hold values from -0.125 to 0.125
- w_down: bfloat16 [5632, 2048], P('col', 'row'), may hold values from -0.078125 to 0.078125
- segments: int32 [4, 2048], P('dp'), may hold values from 0 to 3, never falling along the last dimension, each value on 1 to 1536 neighbouring positions
- cotangent: bfloat16 [8192, 2048], P(('dp', 'col'), 'row'), may hold values from -6 to 6
Outputs:
- output: bfloat16 [8192, 2048], P(('dp', 'col'), 'row')
- input_grad: float32 [8192, 2048], P(('dp', 'col'), 'row')
- w_query_grad: float32 [2048, 2048], P(('row', 'dp'), 'col')
- w_key_grad: float32 [2048, 256], P(('row', 'dp'), 'col')
- w_value_grad: float32 [2048, 256], P(('row', 'dp'), 'col')
- w_out_grad: float32 [2048, 2048], P(('col', 'dp'), 'row')
- w_gate_grad: float32 [2048, 5632], P(('row', 'dp'), 'col')
- w_up_grad: float32 [2048, 5632], P(('row', 'dp'), 'col')
- w_down_grad: float32 [5632, 2048], P(('col', 'dp'), 'row')
- gain_attn_grad: float32 [2048], P(('row', 'dp'))
- gain_mlp_grad: float32 [2048], P(('row', 'dp'))
Inputs may be any that keep to these rules, and one draw needn't show every extreme that they name: `segments`: segment numbers never fall along a sequence; a segment holds 1 to 1536 tokens and one holds exactly that many.
All inputs are finite; a program needn't handle non-finite values.
Results may differ from a plain program's by a relative error of at most 0.035.
Values may be sent and summed in bfloat16 or wider, within the bound.
A program may use at most 320 MiB of HBM per device.

v0:
```python
import jax
import jax.numpy as jnp
from jax import lax
from jax.sharding import PartitionSpec as P

D = 2048
HD = 64


EPSILON = 1e-05
NEG_LARGE = -1e30


def contract(left_side, right_side, left_dim, right_dim):
    return lax.dot_general(
        left_side,
        right_side,
        (((left_dim,), (right_dim,)), ((), ())),
        preferred_element_type=jnp.float32,
    )


def row_total(value):
    return lax.psum(value, "row")


def gather_cols(value):
    return lax.all_gather(value, "col", axis=0, tiled=True)


def gather_rows(value):
    return lax.all_gather(value, "row", axis=0, tiled=True)


def reduce_rows(left_side, weight, weight_dim, result_rows):

    def partial_term(row_start, row_count):
        return contract(left_side, weight, 1, weight_dim)

    return lax.psum_scatter(
        partial_term(jnp.int32(0), result_rows * lax.axis_size("row")).astype(jnp.bfloat16),
        "row",
        scatter_dimension=0,
        tiled=True,
    ).astype(jnp.float32)


def project_rows(left_side, weight, weight_dim, result_rows):
    return reduce_rows(left_side, weight, weight_dim, result_rows)


def reduce_cols(left_side, weight, weight_dim, result_rows):

    def partial_term(row_start, row_count):
        return contract(left_side, weight, 1, weight_dim)

    return lax.psum_scatter(
        partial_term(jnp.int32(0), result_rows * lax.axis_size("col")).astype(jnp.bfloat16),
        "col",
        scatter_dimension=0,
        tiled=True,
    ).astype(jnp.float32)


def key_fold(update_fn, start_state, rotated_keys, values):
    return update_fn(
        start_state,
        (
            lax.all_gather(rotated_keys, "row", axis=0, tiled=True),
            lax.all_gather(values, "row", axis=0, tiled=True),
        ),
        jnp.int32(0),
    )


def seg_positions(segments):
    seq_count, seq_length = segments.shape
    token_index = jnp.arange(seq_length, dtype=jnp.int32)[None, :]
    first_flag = jnp.concatenate(
        [jnp.ones((seq_count, 1), dtype=bool), segments[:, 1:] != segments[:, :-1]], axis=1
    )
    begins = lax.cummax(jnp.where(first_flag, token_index, jnp.zeros_like(token_index)), axis=1)
    return token_index - begins


def rotate(values, cosine_table, sine_table):
    half_width = values.shape[-1] // 2
    first_half = values[..., :half_width]
    second_half = values[..., half_width:]
    cos_part = cosine_table[:, None, :]
    sin_part = sine_table[:, None, :]
    return jnp.concatenate(
        [
            first_half * cos_part - second_half * sin_part,
            second_half * cos_part + first_half * sin_part,
        ],
        axis=-1,
    )


def rms_scale(values):
    sum_squares = row_total(jnp.sum(values * values, axis=1))
    return lax.rsqrt(sum_squares / D + EPSILON)


def norm_back(grad_normed, values, inv_rms, gain):
    x_hat = values * inv_rms[:, None]
    upstream = grad_normed * gain[None, :]
    inner_sum = row_total(jnp.sum(upstream * x_hat, axis=1))
    grad_input = inv_rms[:, None] * (upstream - x_hat * (inner_sum / D)[:, None])
    return (grad_input, jnp.sum(grad_normed * x_hat, axis=0))


def shards(
    tokens,
    gain_attn,
    w_query,
    w_key,
    w_value,
    w_out,
    gain_mlp,
    w_gate,
    w_up,
    w_down,
    segments,
    cotangent,
):
    token_rows = tokens.shape[0]
    group_rows = token_rows * lax.axis_size("col")
    query_rows = group_rows // lax.axis_size("row")
    query_start = lax.axis_index("row") * query_rows
    seq_length = segments.shape[1]
    seg_flat = segments.reshape(-1)
    pos_flat = seg_positions(segments).reshape(-1)
    query_pos = lax.dynamic_slice_in_dim(pos_flat, query_start, query_rows)
    frequency = 10000.0 ** (-(jnp.arange(HD // 2, dtype=jnp.float32) * 2.0 / HD))
    angles = query_pos.astype(jnp.float32)[:, None] * frequency[None, :]
    cosine_table = jnp.cos(angles)
    sine_table = jnp.sin(angles)
    score_scale = HD ** (-0.5)
    query_width = w_query.shape[1]
    key_width = w_key.shape[1]
    head_count = query_width // HD
    groups = key_width // HD
    per_group = head_count // groups
    ff_width = w_gate.shape[1]
    inputs = tokens.astype(jnp.float32)
    scale_attn = rms_scale(inputs)
    gain_one = gain_attn.astype(jnp.float32)
    normed_attn = (inputs * scale_attn[:, None] * gain_one[None, :]).astype(jnp.bfloat16)
    wide_attn = gather_cols(normed_attn)
    w_qkv = jnp.concatenate([w_query, w_key, w_value], axis=1)
    qkv_pre = project_rows(wide_attn, w_qkv, 0, query_rows)
    queries = (
        rotate(
            qkv_pre[:, :query_width].reshape(query_rows, head_count, HD), cosine_table, sine_table
        )
        .astype(jnp.bfloat16)
        .reshape(query_rows, groups, per_group, HD)
    )
    rotated_keys = (
        rotate(
            qkv_pre[:, query_width : query_width + key_width].reshape(query_rows, groups, HD),
            cosine_table,
            sine_table,
        )
        .astype(jnp.bfloat16)
        .reshape(query_rows, key_width)
    )
    values = qkv_pre[:, query_width + key_width :].astype(jnp.bfloat16)
    query_index = query_start + jnp.arange(query_rows, dtype=jnp.int32)
    query_seg = lax.dynamic_slice_in_dim(seg_flat, query_start, query_rows)

    def logits(piece_k):
        key_count = piece_k.shape[0]
        key_index = jnp.arange(key_count, dtype=jnp.int32)
        same_doc = (
            (query_index[:, None] // seq_length == key_index[None, :] // seq_length)
            & (query_seg[:, None] == seg_flat[None, :])
            & (key_index[None, :] <= query_index[:, None])
        )
        visible_mask = same_doc[:, None, None, :]
        raw_score = (
            jnp.einsum(
                "qgpd,kgd->qgpk",
                queries,
                piece_k.reshape(key_count, groups, HD),
                preferred_element_type=jnp.float32,
            )
            * score_scale
        )
        return (jnp.where(visible_mask, raw_score, NEG_LARGE), visible_mask)

    def absorb(state_now, pieces, key_start):
        running_max, running_sum, accumulated = state_now
        piece_k, piece_v = pieces
        key_count = piece_k.shape[0]
        scores_now, visible_mask = logits(piece_k)
        new_max = jnp.maximum(running_max, jnp.max(scores_now, axis=-1))
        exp_weight = jnp.where(visible_mask, jnp.exp(scores_now - new_max[..., None]), 0.0)
        running_sum = jnp.sum(exp_weight, axis=-1)
        accumulated = jnp.einsum(
            "qgpk,kgd->qgpd",
            exp_weight.astype(jnp.bfloat16),
            piece_v.reshape(key_count, groups, HD),
            preferred_element_type=jnp.float32,
        )
        return (new_max, running_sum, accumulated)

    start_state = (
        jnp.full((query_rows, groups, per_group), NEG_LARGE, jnp.float32),
        jnp.zeros((query_rows, groups, per_group), jnp.float32),
        jnp.zeros((query_rows, groups, per_group, HD), jnp.float32),
    )
    running_max, running_sum, accumulated = key_fold(absorb, start_state, rotated_keys, values)
    attended_full = accumulated / running_sum[..., None]
    log_total = running_max + jnp.log(running_sum)
    attended = attended_full.reshape(query_rows, query_width).astype(jnp.bfloat16)
    wide_heads = gather_rows(attended)
    hidden_attn = inputs + reduce_cols(wide_heads, w_out, 0, token_rows)
    scale_mlp = rms_scale(hidden_attn)
    gain_two = gain_mlp.astype(jnp.float32)
    normed_mlp = (hidden_attn * scale_mlp[:, None] * gain_two[None, :]).astype(jnp.bfloat16)
    wide_mlp = gather_cols(normed_mlp)
    w_pair = jnp.concatenate([w_gate, w_up], axis=1)
    pair_pre = project_rows(wide_mlp, w_pair, 0, query_rows)
    gate_pre = pair_pre[:, :ff_width]
    up_pre = pair_pre[:, ff_width:]
    sigmoid_gate = jax.nn.sigmoid(gate_pre)
    hidden = (gate_pre * sigmoid_gate * up_pre).astype(jnp.bfloat16)
    wide_hidden = gather_rows(hidden)
    output = (hidden_attn + reduce_cols(wide_hidden, w_down, 0, token_rows)).astype(jnp.bfloat16)
    grad_out = cotangent.astype(jnp.float32)
    wide_grad = gather_cols(cotangent)
    w_down_grad = contract(wide_hidden, wide_grad, 0, 0)
    grad_hidden = project_rows(wide_grad, w_down, 1, query_rows)
    grad_gate = grad_hidden * up_pre * sigmoid_gate * (1.0 + gate_pre * (1.0 - sigmoid_gate))
    grad_up = grad_hidden * gate_pre * sigmoid_gate
    grad_pair = jnp.concatenate([grad_gate, grad_up], axis=1).astype(jnp.bfloat16)
    wide_pair = gather_rows(grad_pair)
    pair_grad = contract(wide_mlp, wide_pair, 0, 0)
    grad_normed_mlp = reduce_cols(wide_pair, w_pair, 1, token_rows)
    grad_norm_two, gain_mlp_part = norm_back(grad_normed_mlp, hidden_attn, scale_mlp, gain_two)
    grad_resid = grad_out + grad_norm_two
    grad_branch = gather_cols(grad_resid.astype(jnp.bfloat16))
    w_out_grad = contract(wide_heads, grad_branch, 0, 0)
    grad_attended = (
        project_rows(grad_branch, w_out, 1, query_rows)
        .astype(jnp.bfloat16)
        .reshape(query_rows, groups, per_group, HD)
    )
    delta_rows = jnp.sum(grad_attended.astype(jnp.float32) * attended_full, axis=-1)

    def reflect(state_now, pieces, key_start):
        piece_k, piece_v = pieces
        key_count = piece_k.shape[0]
        keys_three = piece_k.reshape(key_count, groups, HD)
        scores_now, visible_mask = logits(piece_k)
        prob_now = jnp.where(visible_mask, jnp.exp(scores_now - log_total[..., None]), 0.0)
        grad_prob = jnp.einsum(
            "qgpd,kgd->qgpk",
            grad_attended,
            piece_v.reshape(key_count, groups, HD),
            preferred_element_type=jnp.float32,
        )
        grad_score = (prob_now * (grad_prob - delta_rows[..., None])).astype(jnp.bfloat16)
        grad_query = score_scale * jnp.einsum(
            "qgpk,kgd->qgpd", grad_score, keys_three, preferred_element_type=jnp.float32
        )
        key_part = score_scale * jnp.einsum(
            "qgpk,qgpd->kgd", grad_score, queries, preferred_element_type=jnp.float32
        ).reshape(key_count, key_width)
        value_part = jnp.einsum(
            "qgpk,qgpd->kgd",
            prob_now.astype(jnp.bfloat16),
            grad_attended,
            preferred_element_type=jnp.float32,
        ).reshape(key_count, key_width)
        return (grad_query, key_part, value_part)

    zero_keys = jnp.zeros((group_rows, key_width), jnp.float32)
    back_state = (jnp.zeros((query_rows, groups, per_group, HD), jnp.float32), zero_keys, zero_keys)
    grad_query, grad_key_all, grad_value_all = key_fold(reflect, back_state, rotated_keys, values)
    grad_key_own, grad_value_own = (
        lax.psum_scatter(
            grad_key_all.astype(jnp.bfloat16), "row", scatter_dimension=0, tiled=True
        ).astype(jnp.float32),
        lax.psum_scatter(
            grad_value_all.astype(jnp.bfloat16), "row", scatter_dimension=0, tiled=True
        ).astype(jnp.float32),
    )
    grad_query_pre = (
        rotate(grad_query.reshape(query_rows, head_count, HD), cosine_table, -sine_table)
        .astype(jnp.bfloat16)
        .reshape(query_rows, query_width)
    )
    grad_key_pre = (
        rotate(grad_key_own.reshape(query_rows, groups, HD), cosine_table, -sine_table)
        .astype(jnp.bfloat16)
        .reshape(query_rows, key_width)
    )
    grad_qkv = jnp.concatenate(
        [grad_query_pre, grad_key_pre, grad_value_own.astype(jnp.bfloat16)], axis=1
    )
    wide_qkv = gather_rows(grad_qkv)
    qkv_grad = contract(wide_attn, wide_qkv, 0, 0)
    grad_normed_attn = reduce_cols(wide_qkv, w_qkv, 1, token_rows)
    grad_norm_one, gain_attn_part = norm_back(grad_normed_attn, inputs, scale_attn, gain_one)
    input_grad = grad_resid + grad_norm_one
    gain_attn_sum, gain_mlp_sum = lax.psum((gain_attn_part, gain_mlp_part), "col")
    all_grads = (
        lax.psum_scatter(
            qkv_grad[:, :query_width].astype(jnp.bfloat16), "dp", scatter_dimension=0, tiled=True
        ).astype(jnp.float32),
        lax.psum_scatter(
            qkv_grad[:, query_width : query_width + key_width].astype(jnp.bfloat16),
            "dp",
            scatter_dimension=0,
            tiled=True,
        ).astype(jnp.float32),
        lax.psum_scatter(
            qkv_grad[:, query_width + key_width :].astype(jnp.bfloat16),
            "dp",
            scatter_dimension=0,
            tiled=True,
        ).astype(jnp.float32),
        lax.psum_scatter(
            w_out_grad.astype(jnp.bfloat16), "dp", scatter_dimension=0, tiled=True
        ).astype(jnp.float32),
        lax.psum_scatter(
            pair_grad[:, :ff_width].astype(jnp.bfloat16), "dp", scatter_dimension=0, tiled=True
        ).astype(jnp.float32),
        lax.psum_scatter(
            pair_grad[:, ff_width:].astype(jnp.bfloat16), "dp", scatter_dimension=0, tiled=True
        ).astype(jnp.float32),
        lax.psum_scatter(
            w_down_grad.astype(jnp.bfloat16), "dp", scatter_dimension=0, tiled=True
        ).astype(jnp.float32),
        lax.psum_scatter(
            gain_attn_sum.astype(jnp.bfloat16), "dp", scatter_dimension=0, tiled=True
        ).astype(jnp.float32),
        lax.psum_scatter(
            gain_mlp_sum.astype(jnp.bfloat16), "dp", scatter_dimension=0, tiled=True
        ).astype(jnp.float32),
    )
    return (
        output,
        input_grad,
        all_grads[0],
        all_grads[1],
        all_grads[2],
        all_grads[3],
        all_grads[4],
        all_grads[5],
        all_grads[6],
        all_grads[7],
        all_grads[8],
    )


def solution(mesh):
    placed = (
        P(("dp", "col"), "row"),
        P("row"),
        P("row", "col"),
        P("row", "col"),
        P("row", "col"),
        P("col", "row"),
        P("row"),
        P("row", "col"),
        P("row", "col"),
        P("col", "row"),
        P("dp", None),
        P(("dp", "col"), "row"),
    )
    return jax.shard_map(
        shards,
        mesh=mesh,
        in_specs=placed,
        out_specs=(
            P(("dp", "col"), "row"),
            P(("dp", "col"), "row"),
            P(("row", "dp"), "col"),
            P(("row", "dp"), "col"),
            P(("row", "dp"), "col"),
            P(("col", "dp"), "row"),
            P(("row", "dp"), "col"),
            P(("row", "dp"), "col"),
            P(("col", "dp"), "row"),
            P(("row", "dp")),
            P(("row", "dp")),
        ),
        check_vma=False,
    )
```

profile of v0, /device:TPU:0, one launch (start us, length us, event | category | flops | bytes accessed | tf_op | source)
XLA Modules:
  0.0 2341.6 jit_solution(13951025512325607753)
XLA Ops:
  9.6 13.6 psum.42
  30.0 27.8 %all-gather.9.cloned.1.call-done = bf16[2048,512]{1,0:T(8,128)(2,1)} async-done(((bf16[1024,512]{1,0:T(8,128)(2,1)}), bf16[2048,512]{1,0:T(8,128)(2,1)}) %all-gather.9.cloned.1.call-update) | async-done | bytes 2097168 | tf_op jit(solution)/shard_map/all_gather | solution.py:28
  57.8 7.2 convolution_convert_fusion.3
  70.2 88.8 %reduce-scatter.18.cloned.1.call-done = bf16[512,1280]{1,0:T(8,128)(2,1)} async-done(((bf16[2048,1280]{1,0:T(8,128)(2,1)}), bf16[512,1280]{1,0:T(8,128)(2,1)}) %reduce-scatter.18.cloned.1.call-update) | async-done | bytes 1310736 | tf_op jit(solution)/shard_map/reduce_scatter | solution.py:40
  160.1 15.7 all_gather.34
  176.9 16.9 all_gather.33
  203.5 23.4 fusion.60
  226.9 21.8 fusion.2
  248.7 25.3 %fusion.61 = (bf16[512,2,8,64]{0,3,2,1:T(8,128)(2,1)}, f32[512,2,8,64]{0,3,2,1:T(8,128)}) fusion(f32[512,2,8]{0,2,1:T(8,128)S(1)} %fusion.2, bf16[2048,2,64,1]{0,2,3,1:T(8,128)(2,1)S(1)} %bitcast.113, f32[512,2,8,2048]{0,3,2,1:T(8,128)} %get-tuple-element.40, f32[512,2,8]{0,2,1:T(8,128)S(1)} %broadcast_maximum_fusion, pred[512,2048]{0,1:T(8,128)(4,1)} %fusion.16), kind=kOutput, calls=%fused_computation.135 | convolution fusion | flops 2198863872 | bytes 71892992 | tf_op jit(solution)/shard_map/qgpk,kgd->qgpd/dot_general | solution.py:202
  274.2 80.5 %all-gather.11.cloned.1.call-done = bf16[2048,1024]{0,1:T(8,128)(2,1)} async-done(((bf16[512,1024]{0,1:T(8,128)(2,1)}), bf16[2048,1024]{0,1:T(8,128)(2,1)}) %all-gather.11.cloned.1.call-update) | async-done | bytes 4194320 | tf_op jit(solution)/shard_map/all_gather | solution.py:32
  354.7 6.2 convolution_convert_fusion.7
  360.9 30.5 %reduce-scatter.20.cloned.1.call-done = bf16[1024,512]{1,0:T(8,128)(2,1)} async-done(((bf16[2048,512]{1,0:T(8,128)(2,1)}), bf16[1024,512]{1,0:T(8,128)(2,1)}) %reduce-scatter.20.cloned.1.call-update) | async-done | bytes 1048592 | tf_op jit(solution)/shard_map/reduce_scatter | solution.py:57
  393.4 11.7 psum.43
  414.7 23.8 %all-gather.13.cloned.1.call-done = bf16[2048,512]{1,0:T(8,128)(2,1)} async-done(((bf16[1024,512]{1,0:T(8,128)(2,1)}), bf16[2048,512]{1,0:T(8,128)(2,1)}) %all-gather.13.cloned.1.call-update) | async-done | bytes 2097168 | tf_op jit(solution)/shard_map/all_gather | solution.py:28
  438.5 19.4 convolution_convert_fusion
  458.0 15.0 all-gather.17.cloned.1.call-done
  473.0 11.1 convolution_convert_fusion.1
  484.2 372.0 %reduce-scatter.22.cloned.1.call-done = bf16[512,5632]{1,0:T(8,128)(2,1)} async-done(((bf16[2048,5632]{1,0:T(8,128)(2,1)}), bf16[512,5632]{1,0:T(8,128)(2,1)}) %reduce-scatter.22.cloned.1.call-update) | async-done | bytes 5767184 | tf_op jit(solution)/shard_map/reduce_scatter | solution.py:40
  856.2 8.3 convert_element_type.202
  864.5 190.7 %reduce-scatter.26.cloned.1.call-done = bf16[512,2816]{1,0:T(8,128)(2,1)} async-done(((bf16[2048,2816]{1,0:T(8,128)(2,1)}), bf16[512,2816]{1,0:T(8,128)(2,1)}) %reduce-scatter.26.cloned.1.call-update) | async-done | bytes 2883600 | tf_op jit(solution)/shard_map/reduce_scatter | solution.py:40
  1055.2 8.0 fusion.13
  1066.3 392.0 %all-gather.19.cloned.1.call-done = bf16[2048,5632]{1,0:T(8,128)(2,1)} async-done(((bf16[512,5632]{1,0:T(8,128)(2,1)}), bf16[2048,5632]{1,0:T(8,128)(2,1)}) %all-gather.19.cloned.1.call-update) | async-done | bytes 23068688 | tf_op jit(solution)/shard_map/all_gather | solution.py:32
  1458.3 19.2 convolution_convert_fusion.6
  1477.5 30.3 %reduce-scatter.28.cloned.1.call-done = bf16[1024,512]{1,0:T(8,128)(2,1)} async-done(((bf16[2048,512]{1,0:T(8,128)(2,1)}), bf16[1024,512]{1,0:T(8,128)(2,1)}) %reduce-scatter.28.cloned.1.call-update) | async-done | bytes 1048592 | tf_op jit(solution)/shard_map/reduce_scatter | solution.py:57
  1511.2 11.7 psum.44
  1526.9 30.4 %all-gather.21.cloned.1.call-done = bf16[2048,512]{1,0:T(8,128)(2,1)} async-done(((bf16[1024,512]{1,0:T(8,128)(2,1)}), bf16[2048,512]{1,0:T(8,128)(2,1)}) %all-gather.21.cloned.1.call-update) | async-done | bytes 2097168 | tf_op jit(solution)/shard_map/all_gather | solution.py:28
  1563.6 76.9 %reduce-scatter.30.cloned.1.call-done = bf16[512,1024]{1,0:T(8,128)(2,1)} async-done(((bf16[2048,1024]{1,0:T(8,128)(2,1)}), bf16[512,1024]{1,0:T(8,128)(2,1)}) %reduce-scatter.30.cloned.1.call-update) | async-done | bytes 1048592 | tf_op jit(solution)/shard_map/reduce_scatter | solution.py:40
  1645.2 38.1 %fusion.1 = bf16[512,2,8,2048]{0,3,2,1:T(8,128)(2,1)} fusion(f32[512,2,8,2048]{0,3,2,1:T(8,128)} %get-tuple-element.40, bf16[2048,2,64,1]{0,2,3,1:T(8,128)(2,1)} %bitcast.112, bf16[512,2,8,64]{0,3,2,1:T(8,128)(2,1)S(1)} %bitcast.100, f32[512,2,8]{0,2,1:T(8,128)S(1)} %multiply_reduce_fusion, f32[512,2,8]{0,2,1:T(8,128)S(1)} %log_add_fusion, ...), kind=kOutput, calls=%fused_computation.2 | convolution fusion | flops 2231369728 | bytes 103350272 | tf_op jit(solution)/shard_map/qgpd,kgd->qgpk/dot_general | solution.py:260
  1683.4 17.1 fusion.31
  1700.7 24.7 %fusion.27 = bf16[2,64,2048]{2,1,0:T(8,128)(2,1)} fusion(bf16[512,2,8,64]{0,3,2,1:T(8,128)(2,1)} %bitcast.99, f32[512,2,8,2048]{0,3,2,1:T(8,128)} %get-tuple-element.40, f32[512,2,8]{0,2,1:T(8,128)S(1)} %log_add_fusion, pred[512,2048]{0,1:T(8,128)(4,1)} %fusion.16), kind=kOutput, calls=%fused_computation.51 | convolution fusion | flops 2198077440 | bytes 69763072 | tf_op jit(solution)/shard_map/qgpk,qgpd->kgd/dot_general | solution.py:273
  1726.5 13.6 convolution_multiply_fusion
  1750.5 198.2 %all-gather.15.cloned.1.call-done = bf16[2048,2816]{1,0:T(8,128)(2,1)} async-done(((bf16[512,2816]{1,0:T(8,128)(2,1)}), bf16[2048,2816]{1,0:T(8,128)(2,1)}) %all-gather.15.cloned.1.call-update) | async-done | bytes 11534352 | tf_op jit(solution)/shard_map/all_gather | solution.py:32
  1948.8 10.8 convolution_convert_fusion.4
  1960.0 17.3 convolution_convert_fusion.2
  1981.0 6.2 convolution_convert_fusion.11
  1987.3 59.7 %all-gather.23.cloned.1.call-done = bf16[2048,1280]{0,1:T(8,128)(2,1)} async-done(((bf16[512,1280]{0,1:T(8,128)(2,1)}), bf16[2048,1280]{0,1:T(8,128)(2,1)}) %all-gather.23.cloned.1.call-update) | async-done | bytes 5242896 | tf_op jit(solution)/shard_map/all_gather | solution.py:32
  2058.3 7.1 convolution_convert_fusion.9
  2065.5 9.9 convolution_convert_fusion.10
  2076.7 7.2 reduce-scatter.50.cloned.1.call-done
  2086.4 36.2 %reduce-scatter.46.cloned.1.call-done = bf16[128,2816]{1,0:T(8,128)(2,1)} async-done(((bf16[512,2816]{1,0:T(8,128)(2,1)}), bf16[128,2816]{1,0:T(8,128)(2,1)}) %reduce-scatter.46.cloned.1.call-update) | async-done | bytes 720912 | tf_op jit(solution)/shard_map/reduce_scatter | solution.py:330
  2124.9 36.5 %reduce-scatter.48.cloned.1.call-done = bf16[128,2816]{1,0:T(8,128)(2,1)} async-done(((bf16[512,2816]{1,0:T(8,128)(2,1)}), bf16[128,2816]{1,0:T(8,128)(2,1)}) %reduce-scatter.48.cloned.1.call-update) | async-done | bytes 720912 | tf_op jit(solution)/shard_map/reduce_scatter | solution.py:333
  2163.7 24.9 %reduce-scatter.44.cloned.1.call-done = bf16[256,512]{1,0:T(8,128)(2,1)} async-done(((bf16[1024,512]{1,0:T(8,128)(2,1)}), bf16[256,512]{1,0:T(8,128)(2,1)}) %reduce-scatter.44.cloned.1.call-update) | async-done | bytes 262160 | tf_op jit(solution)/shard_map/reduce_scatter | solution.py:327
  2190.4 20.3 reduce-scatter.40.cloned.1.call-done
  2212.1 21.3 reduce-scatter.42.cloned.1.call-done
  2234.7 26.6 %reduce-scatter.38.cloned.1.call-done = bf16[128,1024]{1,0:T(8,128)(2,1)} async-done(((bf16[512,1024]{1,0:T(8,128)(2,1)}), bf16[128,1024]{1,0:T(8,128)(2,1)}) %reduce-scatter.38.cloned.1.call-update) | async-done | bytes 262160 | tf_op jit(solution)/shard_map/reduce_scatter | solution.py:312
  2263.1 32.8 %reduce-scatter.36.cloned.1.call-done = bf16[1024,512]{1,0:T(8,128)(2,1)} async-done(((bf16[2048,512]{1,0:T(8,128)(2,1)}), bf16[1024,512]{1,0:T(8,128)(2,1)}) %reduce-scatter.36.cloned.1.call-update) | async-done | bytes 1048592 | tf_op jit(solution)/shard_map/reduce_scatter | solution.py:57
  2309.2 11.3 psum.45
  2321.7 8.4 reduce-scatter.24.cloned.1.call-done
  (184 shorter events, 119.9 us)
Async XLA Ops:
  7.2 465.8 %copy-start = (bf16[2816,512]{1,0:T(8,128)(2,1)S(1)}, bf16[2816,512]{1,0:T(8,128)(2,1)}, u32[]{:S(2)}) copy-start(bf16[2816,512]{1,0:T(8,128)(2,1)} %param.21) | copy-start | bytes 8650756
  7.2 50.6 %all-gather.9.cloned.1.call-start = ((), (), s32[]{:S(2)}) async-start(), calls=%async_computation.17 | async-start | bytes 3145728 | tf_op jit(solution)/shard_map/all_gather | solution.py:28
  8.1 20.6 copy-start.26
  9.6 19.1 copy-start.15
  9.6 19.8 copy-start.16
  26.4 132.6 %reduce-scatter.18.cloned.1.call-start = ((), (), s32[]{:S(2)}) async-start(), calls=%async_computation.18 | async-start | bytes 6553600 | tf_op jit(solution)/shard_map/reduce_scatter | solution.py:40
  65.0 289.6 %all-gather.11.cloned.1.call-start = ((), (), s32[]{:S(2)}) async-start(), calls=%async_computation.19 | async-start | bytes 5242880 | tf_op jit(solution)/shard_map/all_gather | solution.py:32
  67.7 133.9 %copy-start.10 = (f32[512,32]{0,1:T(8,128)}, f32[512,32]{0,1:T(8,128)S(1)}, u32[]{:S(2)}) copy-start(f32[512,32]{0,1:T(8,128)S(1)} %get-tuple-element.38) | copy-start | bytes 196612
  175.8 27.7 %copy-start.8 = (bf16[2048,128]{0,1:T(8,128)(2,1)}, bf16[2048,128]{0,1:T(8,128)(2,1)S(1)}, u32[]{:S(2)}) copy-start(bf16[2048,128]{0,1:T(8,128)(2,1)S(1)} %all_gather.34) | copy-start | bytes 1572868
  203.5 23.4 %copy-start.5 = (bf16[512,16,32]{0,2,1:T(8,128)(2,1)}, bf16[512,16,32]{0,2,1:T(8,128)(2,1)S(1)}, u32[]{:S(2)}) copy-start(bf16[512,16,32]{0,2,1:T(8,128)(2,1)S(1)} %get-tuple-element.26) | copy-start | bytes 1572868
  203.5 23.4 copy-start.7
  226.9 21.8 copy-start.14
  274.1 86.8 %copy-start.29 = (bf16[512]{0:T(512)(128)(2,1)S(1)}, bf16[512]{0:T(512)(128)(2,1)}, u32[]{:S(2)}) copy-start(bf16[512]{0:T(512)(128)(2,1)} %param.18) | copy-start | bytes 3076
  274.1 117.3 %reduce-scatter.20.cloned.1.call-start = ((), (), s32[]{:S(2)}) async-start(), calls=%async_computation.20 | async-start | bytes 3145728 | tf_op jit(solution)/shard_map/reduce_scatter | solution.py:57
  360.9 77.6 %all-gather.13.cloned.1.call-start = ((), (), s32[]{:S(2)}) async-start(), calls=%async_computation.21 | async-start | bytes 3145728 | tf_op jit(solution)/shard_map/all_gather | solution.py:28
  360.9 1161.9 %copy-start.22 = (f32[512]{0:T(512)}, f32[512]{0:T(512)S(1)}, u32[]{:S(2)}) copy-start(f32[512]{0:T(512)S(1)} %convert_element_type.199) | copy-start | bytes 6148
  405.1 1117.8 %copy-start.17 = (f32[1024]{0:T(1024)}, f32[1024]{0:T(1024)S(1)}, u32[]{:S(2)}) copy-start(f32[1024]{0:T(1024)S(1)} %add_rsqrt_fusion) | copy-start | bytes 12292
  408.0 65.0 %all-gather.17.cloned.1.call-start = ((), (), s32[]{:S(2)}) async-start(), calls=%async_computation.25 | async-start | bytes 3145728 | tf_op jit(solution)/shard_map/all_gather | solution.py:28
  408.6 447.6 %reduce-scatter.22.cloned.1.call-start = ((), (), s32[]{:S(2)}) async-start(), calls=%async_computation.22 | async-start | bytes 28835840 | tf_op jit(solution)/shard_map/reduce_scatter | solution.py:40
  458.0 597.2 %reduce-scatter.26.cloned.1.call-start = ((), (), s32[]{:S(2)}) async-start(), calls=%async_computation.26 | async-start | bytes 14417920 | tf_op jit(solution)/shard_map/reduce_scatter | solution.py:40
  484.2 974.1 %all-gather.19.cloned.1.call-start = ((), (), s32[]{:S(2)}) async-start(), calls=%async_computation.27 | async-start | bytes 28835840 | tf_op jit(solution)/shard_map/all_gather | solution.py:32
  1066.0 441.8 %reduce-scatter.28.cloned.1.call-start = ((), (), s32[]{:S(2)}) async-start(), calls=%async_computation.28 | async-start | bytes 3145728 | tf_op jit(solution)/shard_map/reduce_scatter | solution.py:57
  1477.5 79.9 %all-gather.21.cloned.1.call-start = ((), (), s32[]{:S(2)}) async-start(), calls=%async_computation.29 | async-start | bytes 3145728 | tf_op jit(solution)/shard_map/all_gather | solution.py:28
  1522.9 4.0 copy-start.24
  1526.9 113.6 %reduce-scatter.30.cloned.1.call-start = ((), (), s32[]{:S(2)}) async-start(), calls=%async_computation.30 | async-start | bytes 5242880 | tf_op jit(solution)/shard_map/reduce_scatter | solution.py:40
  1563.5 178.0 %reduce-scatter.32.cloned.1.call-start = ((), (), s32[]{:S(2)}) async-start(), calls=%async_computation.31 | async-start | bytes 655360 | tf_op jit(solution)/shard_map/reduce_scatter | solution.py:285
  1645.2 38.1 %copy-start.6 = (bf16[512,16,32]{0,2,1:T(8,128)(2,1)S(1)}, bf16[512,16,32]{0,2,1:T(8,128)(2,1)}, u32[]{:S(2)}) copy-start(bf16[512,16,32]{0,2,1:T(8,128)(2,1)} %copy-done.5) | copy-start | bytes 1572868
  1700.5 47.5 %reduce-scatter.34.cloned.1.call-start = ((), (), s32[]{:S(2)}) async-start(), calls=%async_computation.32 | async-start | bytes 655360 | tf_op jit(solution)/shard_map/reduce_scatter | solution.py:288
  1725.4 223.3 %all-gather.15.cloned.1.call-start = ((), (), s32[]{:S(2)}) async-start(), calls=%async_computation.23 | async-start | bytes 14417920 | tf_op jit(solution)/shard_map/all_gather | solution.py:32
  1726.0 14.1 copy-start.11
  1726.0 14.1 copy-start.13
  1726.1 321.0 %all-gather.23.cloned.1.call-start = ((), (), s32[]{:S(2)}) async-start(), calls=%async_computation.33 | async-start | bytes 6553600 | tf_op jit(solution)/shard_map/all_gather | solution.py:32
  1750.5 333.5 %reduce-scatter.50.cloned.1.call-start = ((), (), s32[]{:S(2)}) async-start(), calls=%async_computation.41 | async-start | bytes 3604480 | tf_op jit(solution)/shard_map/reduce_scatter | solution.py:336
  1959.5 163.0 %reduce-scatter.46.cloned.1.call-start = ((), (), s32[]{:S(2)}) async-start(), calls=%async_computation.39 | async-start | bytes 3604480 | tf_op jit(solution)/shard_map/reduce_scatter | solution.py:330
  1980.2 181.1 %reduce-scatter.48.cloned.1.call-start = ((), (), s32[]{:S(2)}) async-start(), calls=%async_computation.40 | async-start | bytes 3604480 | tf_op jit(solution)/shard_map/reduce_scatter | solution.py:333
  1981.0 207.6 %reduce-scatter.44.cloned.1.call-start = ((), (), s32[]{:S(2)}) async-start(), calls=%async_computation.38 | async-start | bytes 1310720 | tf_op jit(solution)/shard_map/reduce_scatter | solution.py:327
  1987.3 223.4 %reduce-scatter.40.cloned.1.call-start = ((), (), s32[]{:S(2)}) async-start(), calls=%async_computation.36 | async-start | bytes 163840 | tf_op jit(solution)/shard_map/reduce_scatter | solution.py:315
  2054.9 178.5 %reduce-scatter.42.cloned.1.call-start = ((), (), s32[]{:S(2)}) async-start(), calls=%async_computation.37 | async-start | bytes 163840 | tf_op jit(solution)/shard_map/reduce_scatter | solution.py:321
  2055.6 205.7 %reduce-scatter.38.cloned.1.call-start = ((), (), s32[]{:S(2)}) async-start(), calls=%async_computation.35 | async-start | bytes 1310720 | tf_op jit(solution)/shard_map/reduce_scatter | solution.py:312
  2058.1 237.8 %reduce-scatter.36.cloned.1.call-start = ((), (), s32[]{:S(2)}) async-start(), calls=%async_computation.34 | async-start | bytes 3145728 | tf_op jit(solution)/shard_map/reduce_scatter | solution.py:57
  2065.5 10.0 copy-start.30
  2065.5 264.6 %reduce-scatter.24.cloned.1.call-start = ((), (), s32[]{:S(2)}) async-start(), calls=%async_computation.24 | async-start | bytes 3145728 | tf_op jit(solution)/shard_map/reduce_scatter | solution.py:57
  2086.4 209.5 %copy-start.21 = (f32[1024]{0:T(1024)S(1)}, f32[1024]{0:T(1024)}, u32[]{:S(2)}) copy-start(f32[1024]{0:T(1024)} %copy-done.20) | copy-start | bytes 12292
  2086.4 209.5 %copy-start.27 = (f32[512]{0:T(512)S(1)}, f32[512]{0:T(512)}, u32[]{:S(2)}) copy-start(f32[512]{0:T(512)} %copy-done.26) | copy-start | bytes 6148
  2124.9 173.4 %copy-start.28 = (f32[512]{0:T(512)S(1)}, f32[512]{0:T(512)}, u32[]{:S(2)}) copy-start(f32[512]{0:T(512)} %get-tuple-element.11) | copy-start | bytes 6148
  2124.9 205.2 %copy-start.18 = (f32[1024]{0:T(1024)S(1)}, f32[1024]{0:T(1024)}, u32[]{:S(2)}) copy-start(f32[1024]{0:T(1024)} %copy-done.17) | copy-start | bytes 12292
  2124.9 205.2 %copy-start.23 = (f32[512]{0:T(512)S(1)}, f32[512]{0:T(512)}, u32[]{:S(2)}) copy-start(f32[512]{0:T(512)} %copy-done.22) | copy-start | bytes 6148
  2124.9 205.2 %copy-start.25 = (f32[1024]{0:T(1024)S(1)}, f32[1024]{0:T(1024)}, u32[]{:S(2)}) copy-start(f32[1024]{0:T(1024)} %copy-done.24) | copy-start | bytes 12292
  (8 other events, 14.1 us)
Sparse Core Ops, SparseCore 0:
  26.5 31.2 all-gather.8
  65.1 93.7 reduce-scatter.17
  274.2 80.3 all-gather.10
  361.0 30.3 reduce-scatter.19
  408.1 30.3 all-gather.12
  439.9 33.0 all-gather.16
  475.4 380.7 reduce-scatter.21
  858.6 196.5 reduce-scatter.25
  1066.2 392.0 all-gather.18
  1477.6 30.1 reduce-scatter.27
  1527.0 30.3 all-gather.20
  1563.7 76.7 reduce-scatter.29
  1700.6 22.3 reduce-scatter.31
  1725.7 22.2 reduce-scatter.33
  1749.4 199.2 all-gather.14
  1950.8 96.2 all-gather.22
  2049.4 34.5 reduce-scatter.49
  2086.3 36.1 reduce-scatter.45
  2125.1 36.1 reduce-scatter.47
  2163.7 24.8 reduce-scatter.43
  2191.0 19.6 reduce-scatter.39
  2213.7 19.6 reduce-scatter.41
  2236.4 24.8 reduce-scatter.37
  2263.9 31.8 reduce-scatter.35
  2298.1 31.8 reduce-scatter.23
where the time goes:
time: 2350 us; the launch traced here: 2340 us
  waiting for transfers between devices  1840 us (78%)
  matrix products  269 us (11%)
  other arithmetic  93 us (4%)
  blocking collectives  91.9 us (4%)
  local copies, waits for them, and re-layouts  30.9 us (1%)
    all_gather x4, waiting for transfers between devices, gather_rows(): return lax.all_gather(value, 'row', axis=0, tiled=True)  730 us
    reduce_scatter x4, waiting for transfers between devices, reduce_rows(): lax.psum_scatter(partial_term(jnp.int32(0), result_rows * lax.axis_size('...  728 us
    dot_general x12, matrix products, contract(): lax.dot_general(left_side, right_side, (((left_dim,), (right_dim,)), ((),...  127 us
    reduce_scatter x4, waiting for transfers between devices, reduce_cols(): lax.psum_scatter(partial_term(jnp.int32(0), result_rows * lax.axis_size('...  102 us
    all_gather x4, waiting for transfers between devices, gather_cols(): return lax.all_gather(value, 'col', axis=0, tiled=True)  97 us
    psum x4, blocking collectives, row_total(): return lax.psum(value, 'row')  48.3 us
  transfers between devices with their start and end apart: 25, of which 24 were waited for; matrix products, arithmetic and copies ran while one was open for 8% of the time, Pallas kernels for 0%

commit v1 on v0

v1 whole, which is shorter than its diff:
```python
import jax
import jax.numpy as jnp
from jax import lax
from jax.sharding import PartitionSpec as P

D = 2048
HD = 64
EPSILON = 1e-05
NEG_LARGE = -1e30
BF = jnp.bfloat16
F32 = jnp.float32


def contract(left_side, right_side, left_dim, right_dim):
    return lax.dot_general(
        left_side,
        right_side,
        (((left_dim,), (right_dim,)), ((), ())),
        preferred_element_type=F32,
    )


def cat(parts, axis=0):
    return jnp.concatenate(parts, axis=axis)


def either(flag, first, second):
    return jnp.where(flag == 0, first, second)


def seg_positions(segments):
    seq_count, seq_length = segments.shape
    token_index = jnp.arange(seq_length, dtype=jnp.int32)[None, :]
    first_flag = jnp.concatenate(
        [jnp.ones((seq_count, 1), dtype=bool), segments[:, 1:] != segments[:, :-1]], axis=1
    )
    begins = lax.cummax(jnp.where(first_flag, token_index, jnp.zeros_like(token_index)), axis=1)
    return token_index - begins


def rotate(values, cosine_table, sine_table):
    half_width = values.shape[-1] // 2
    first_half = values[..., :half_width]
    second_half = values[..., half_width:]
    cos_part = cosine_table[:, None, :]
    sin_part = sine_table[:, None, :]
    return jnp.concatenate(
        [
            first_half * cos_part - second_half * sin_part,
            second_half * cos_part + first_half * sin_part,
        ],
        axis=-1,
    )


def rms_scale(values):
    return lax.rsqrt(jnp.sum(values * values, axis=1) / D + EPSILON)


def norm_back(grad_normed, values, inv_rms, gain):
    x_hat = values * inv_rms[:, None]
    upstream = grad_normed * gain[None, :]
    inner_sum = jnp.sum(upstream * x_hat, axis=1)
    grad_input = inv_rms[:, None] * (upstream - x_hat * (inner_sum / D)[:, None])
    return (grad_input, jnp.sum(grad_normed * x_hat, axis=0))


def shards(
    tokens,
    gain_attn,
    w_query,
    w_key,
    w_value,
    w_out,
    gain_mlp,
    w_gate,
    w_up,
    w_down,
    segments,
    cotangent,
):
    rows = lax.axis_size("row")
    dp_size = lax.axis_size("dp")
    spans = dp_size // 4
    assert lax.axis_size("col") == 2 and dp_size % 4 == 0 and segments.shape[0] == 1
    row_at = lax.axis_index("row")
    col_at = lax.axis_index("col")
    dp_at = lax.axis_index("dp")
    core_at = dp_at % 2
    y_at = (dp_at // 2) % 2
    token_half = tokens.shape[0]
    own_tokens = token_half // rows
    block = own_tokens // 2
    feat = tokens.shape[1]
    half_feat = feat // 2
    seq_length = segments.shape[1]
    wide = rows * half_feat

    swap_core = [(i, i ^ 1) for i in range(dp_size)]
    swap_y = [(i, i ^ 2) for i in range(dp_size)]

    def from_core(v):
        return lax.ppermute(v, "dp", swap_core)

    def from_y(v):
        return lax.ppermute(v, "dp", swap_y)

    def from_x(v):
        return lax.ppermute(v, "col", [(0, 1), (1, 0)])

    def own_y(v):
        parts = v.reshape((spans, 2, feat // (2 * spans)) + v.shape[1:])
        return lax.dynamic_index_in_dim(parts, y_at, 1, keepdims=False).reshape(
            (half_feat,) + v.shape[1:]
        )

    def y_order(v):
        parts = v.reshape(v.shape[0], spans, 2, feat // (2 * spans))
        low = parts[:, :, 0].reshape(v.shape[0], half_feat)
        high = parts[:, :, 1].reshape(v.shape[0], half_feat)
        return cat([either(y_at, low, high), either(y_at, high, low)], axis=1)

    def y_restore(v):
        own, other = v[:, :half_feat], v[:, half_feat:]
        low, high = either(y_at, own, other), either(y_at, other, own)
        shape = (v.shape[0], spans, 1, feat // (2 * spans))
        return cat([low.reshape(shape), high.reshape(shape)], axis=2).reshape(v.shape)

    def deal(v):
        parts = v.reshape(2, rows, block, v.shape[1])
        return jnp.stack([parts[0], parts[1, ::-1]], axis=1)

    def undeal(v):
        parts = v.reshape(rows, 2, block, v.shape[-1])
        return cat([parts[:, 0], parts[::-1, 1]]).reshape(token_half, v.shape[-1])

    def to_tokens(v):
        sent = deal(y_order(v)).reshape(rows, own_tokens, feat)
        came = lax.all_to_all(sent, "row", split_axis=0, concat_axis=0, tiled=True)
        came = came.reshape(rows, own_tokens, 2, half_feat)
        return came.transpose(1, 2, 0, 3).reshape(own_tokens, 2 * wide)

    def to_features(v):
        sent = v.astype(BF).reshape(own_tokens, 2, rows, half_feat)
        sent = sent.transpose(2, 0, 1, 3).reshape(rows, own_tokens, feat)
        came = lax.all_to_all(sent, "row", split_axis=0, concat_axis=0, tiled=True)
        return y_restore(undeal(came))

    def spread(v):
        across = from_x(v)
        return cat([v, across, from_core(v), from_core(across)])

    def fold(v):
        count = v.shape[0]
        summed = v[: count // 2] + from_core(v[count // 2 :].astype(BF)).astype(F32)
        return summed[: count // 4] + from_x(summed[count // 4 :].astype(BF)).astype(F32)

    def core_cols(v):
        parts = v.reshape(v.shape[0], 2, v.shape[1] // 2)
        return lax.dynamic_index_in_dim(parts, core_at, 1, keepdims=False)

    def core_rows(v):
        parts = v.reshape(2, v.shape[0] // 2, v.shape[1])
        return lax.dynamic_index_in_dim(parts, core_at, 0, keepdims=False)

    def fetch(piece):
        own = lax.all_gather(piece, "row", axis=0, tiled=True)
        return own, from_y(own)

    def ahead(left_side, weight):
        return contract(left_side[:, :wide], weight[0], 1, 0) + contract(
            left_side[:, wide:], weight[1], 1, 0
        )

    def back(left_side, weight):
        return cat(
            [contract(left_side, weight[0], 1, 1), contract(left_side, weight[1], 1, 1)], axis=1
        )

    def weight_grad(left_side, right_side):
        away = contract(left_side[:, wide:], right_side, 0, 0).astype(BF)
        kept = contract(left_side[:, :wide], right_side, 0, 0) + from_y(away).astype(F32)
        return lax.psum_scatter(kept.astype(BF), "row", scatter_dimension=0, tiled=True)

    span_groups = [[low + 4 * high for high in range(spans)] for low in range(4)]
    near_groups = [[4 * high + low for low in range(4)] for high in range(spans)]

    def finish_rows(tile):
        count = tile.shape[1]
        if spans > 1:
            tile = lax.psum_scatter(
                tile, "dp", scatter_dimension=0, tiled=True, axis_index_groups=span_groups
            )
        parts = tile.reshape(2, tile.shape[0] // 2, count)
        own = lax.dynamic_index_in_dim(parts, core_at, 0, keepdims=False)
        other = from_core(lax.dynamic_index_in_dim(parts, 1 - core_at, 0, keepdims=False))
        return lambda start, stop: cat(
            [
                either(core_at, own, other)[:, start:stop],
                either(core_at, other, own)[:, start:stop],
            ],
            axis=1,
        ).astype(F32)

    def finish_cols(tile):
        flipped = tile.T
        count = flipped.shape[0]
        if spans > 1:
            every = lax.all_gather(
                flipped, "dp", axis=0, tiled=False, axis_index_groups=near_groups
            ).reshape(2, 2, count, spans, half_feat // spans)
            whole = every.transpose(1, 2, 3, 0, 4).reshape(spans, 4, -1, feat)
            mine = lax.dynamic_index_in_dim(whole, dp_at % 4, 1, keepdims=False)
            return lax.psum_scatter(
                mine.reshape(-1, feat),
                "dp",
                scatter_dimension=0,
                tiled=True,
                axis_index_groups=span_groups,
            ).astype(F32)
        parts = flipped.reshape(2, count // 2, half_feat)
        same = lax.dynamic_index_in_dim(parts, y_at, 0, keepdims=False)
        cross = lax.dynamic_index_in_dim(parts, 1 - y_at, 0, keepdims=False)
        perm_same = [(2 * a + b, 2 * b + a) for a in range(2) for b in range(2)]
        perm_cross = [(2 * a + b, 2 * b + 1 - a) for a in range(2) for b in range(2)]
        first = lax.ppermute(same, "dp", perm_same)
        second = lax.ppermute(cross, "dp", perm_cross)
        return cat(
            [either(core_at, first, second), either(core_at, second, first)], axis=1
        ).astype(F32)

    query_width = w_query.shape[1] // 2
    key_width = w_key.shape[1] // 2
    ff_width = w_gate.shape[1] // 2
    heads = query_width // HD
    assert key_width == HD
    qkv_piece = cat(
        [core_cols(own_y(w_query)), core_cols(own_y(w_key)), core_cols(own_y(w_value))], axis=1
    )
    w_qkv = fetch(qkv_piece)
    w_out_t = fetch(own_y(core_rows(w_out).T))
    w_gate_b = fetch(core_cols(own_y(w_gate)))
    w_up_b = fetch(core_cols(own_y(w_up)))
    w_down_t = fetch(own_y(core_rows(w_down).T))

    both = cat([segments, from_core(segments)])
    placed = seg_positions(both)

    def dealt_index(row_index):
        cols = jnp.stack([col_at, 1 - col_at])[:, None] * (2 * rows)
        return (cols + jnp.stack([row_index, 2 * rows - 1 - row_index])[None, :]).reshape(-1)

    def picked(table, index):
        return table.reshape(2, 4 * rows, block)[:, index].reshape(2, -1)

    key_blocks = cat([dealt_index((row_at + j) % rows) for j in range(rows)])
    query_blocks = key_blocks[:4]
    spot = jnp.broadcast_to(jnp.arange(seq_length, dtype=jnp.int32)[None, :], (2, seq_length))
    query_spot, key_spot = picked(spot, query_blocks), picked(spot, key_blocks)
    query_seg, key_seg = picked(both, query_blocks), picked(both, key_blocks)
    query_pos = picked(placed, query_blocks).reshape(-1)
    frequency = 10000.0 ** (-(jnp.arange(HD // 2, dtype=F32) * 2.0 / HD))
    angles = query_pos.astype(F32)[:, None] * frequency[None, :]
    cosine_table = jnp.cos(angles)
    sine_table = jnp.sin(angles)
    score_scale = HD ** (-0.5)

    gains = lax.all_gather(
        y_order(jnp.stack([gain_attn, gain_mlp])).reshape(2, 2, half_feat), "row", axis=2
    ).reshape(2, 2 * wide)
    gain_one = gains[0].astype(F32)
    gain_two = gains[1].astype(F32)

    inputs = to_tokens(tokens).astype(F32)
    scale_attn = rms_scale(inputs)
    normed_attn = (inputs * scale_attn[:, None] * gain_one[None, :]).astype(BF)
    wide_attn = spread(normed_attn)
    count = wide_attn.shape[0]
    per_seq = count // 2
    qkv_pre = ahead(wide_attn, w_qkv)
    queries = (
        rotate(qkv_pre[:, :query_width].reshape(count, heads, HD), cosine_table, sine_table)
        .astype(BF)
        .reshape(2, per_seq, heads, HD)
    )
    keys_here = rotate(
        qkv_pre[:, query_width : query_width + HD].reshape(count, 1, HD), cosine_table, sine_table
    ).reshape(count, HD)
    kv_here = cat([keys_here, qkv_pre[:, query_width + HD :]], axis=1).astype(BF)

    def row_shift(j):
        return [(s, (s - j) % rows) for s in range(rows)]

    def row_return(j):
        return [(s, (s + j) % rows) for s in range(rows)]

    kv_all = jnp.stack(
        [kv_here.reshape(2, per_seq, 2 * HD)]
        + [
            lax.ppermute(kv_here, "row", row_shift(j)).reshape(2, per_seq, 2 * HD)
            for j in range(1, rows)
        ],
        axis=1,
    ).reshape(2, seq_length, 2 * HD)
    keys_all = kv_all[..., :HD]
    values_all = kv_all[..., HD:]
    visible = (
        (query_seg[:, :, None] == key_seg[:, None, :])
        & (key_spot[:, None, :] <= query_spot[:, :, None])
    )[:, :, None, :]

    def logits():
        raw = (
            jnp.einsum("bqhd,bkd->bqhk", queries, keys_all, preferred_element_type=F32)
            * score_scale
        )
        return jnp.where(visible, raw, NEG_LARGE)

    scores = logits()
    top = jnp.max(scores, axis=-1)
    exp_weight = jnp.where(visible, jnp.exp(scores - top[..., None]), 0.0)
    total = jnp.sum(exp_weight, axis=-1)
    attended_full = (
        jnp.einsum("bqhk,bkd->bqhd", exp_weight.astype(BF), values_all, preferred_element_type=F32)
        / total[..., None]
    )
    log_total = top + jnp.log(total)
    attended = attended_full.reshape(count, query_width).astype(BF)

    hidden_attn = inputs + fold(back(attended, w_out_t))
    scale_mlp = rms_scale(hidden_attn)
    normed_mlp = (hidden_attn * scale_mlp[:, None] * gain_two[None, :]).astype(BF)
    wide_mlp = spread(normed_mlp)
    gate_pre = ahead(wide_mlp, w_gate_b)
    up_pre = ahead(wide_mlp, w_up_b)
    sigmoid_gate = jax.nn.sigmoid(gate_pre)
    hidden = (gate_pre * sigmoid_gate * up_pre).astype(BF)
    output = to_features(hidden_attn + fold(back(hidden, w_down_t)))

    cot_tokens = to_tokens(cotangent)
    wide_cot = spread(cot_tokens)
    down_tile = weight_grad(wide_cot, hidden)
    grad_hidden = ahead(wide_cot, w_down_t)
    grad_gate = (
        grad_hidden * up_pre * sigmoid_gate * (1.0 + gate_pre * (1.0 - sigmoid_gate))
    ).astype(BF)
    grad_up = (grad_hidden * gate_pre * sigmoid_gate).astype(BF)
    gate_tile = weight_grad(wide_mlp, grad_gate)
    up_tile = weight_grad(wide_mlp, grad_up)
    grad_normed_mlp = fold(back(grad_gate, w_gate_b) + back(grad_up, w_up_b))
    grad_norm_two, gain_mlp_part = norm_back(grad_normed_mlp, hidden_attn, scale_mlp, gain_two)
    grad_resid = cot_tokens.astype(F32) + grad_norm_two
    wide_branch = spread(grad_resid.astype(BF))
    out_tile = weight_grad(wide_branch, attended)
    grad_attended = ahead(wide_branch, w_out_t).astype(BF).reshape(2, per_seq, heads, HD)
    delta = jnp.sum(grad_attended.astype(F32) * attended_full, axis=-1)

    probs = jnp.where(visible, jnp.exp(logits() - log_total[..., None]), 0.0)
    grad_probs = jnp.einsum(
        "bqhd,bkd->bqhk", grad_attended, values_all, preferred_element_type=F32
    )
    grad_scores = (probs * (grad_probs - delta[..., None])).astype(BF)
    grad_query = score_scale * jnp.einsum(
        "bqhk,bkd->bqhd", grad_scores, keys_all, preferred_element_type=F32
    )
    grad_keys_all = score_scale * jnp.einsum(
        "bqhk,bqhd->bkd", grad_scores, queries, preferred_element_type=F32
    )
    grad_values_all = jnp.einsum(
        "bqhk,bqhd->bkd", probs.astype(BF), grad_attended, preferred_element_type=F32
    )
    grad_kv = cat([grad_keys_all, grad_values_all], axis=2).reshape(2, rows, per_seq, 2 * HD)
    grad_kv_here = grad_kv[:, 0].reshape(count, 2 * HD)
    for j in range(1, rows):
        sent = grad_kv[:, j].reshape(count, 2 * HD).astype(BF)
        grad_kv_here = grad_kv_here + lax.ppermute(sent, "row", row_return(j)).astype(F32)
    grad_query_pre = rotate(
        grad_query.reshape(count, heads, HD), cosine_table, -sine_table
    ).reshape(count, query_width)
    grad_key_pre = rotate(
        grad_kv_here[:, :HD].reshape(count, 1, HD), cosine_table, -sine_table
    ).reshape(count, HD)
    grad_qkv = cat([grad_query_pre, grad_key_pre, grad_kv_here[:, HD:]], axis=1).astype(BF)
    qkv_tile = weight_grad(wide_attn, grad_qkv)
    grad_normed_attn = fold(back(grad_qkv, w_qkv))
    grad_norm_one, gain_attn_part = norm_back(grad_normed_attn, inputs, scale_attn, gain_one)
    input_grad = to_features(grad_resid + grad_norm_one).astype(F32)

    gain_sums = jnp.stack([gain_attn_part, gain_mlp_part]).reshape(2, 2, rows, half_feat)
    gain_sums = gain_sums.transpose(2, 0, 1, 3)
    gain_mine = lax.psum_scatter(gain_sums, "row", scatter_dimension=0, tiled=True)
    gain_rows = y_restore(gain_mine.reshape(2, feat))
    gain_rows = lax.psum(gain_rows, ("dp", "col")).reshape(2, dp_size, feat // dp_size)
    gain_out = lax.dynamic_index_in_dim(gain_rows, dp_at, 1, keepdims=False)

    qkv_part = finish_rows(qkv_tile)
    return (
        output,
        input_grad,
        qkv_part(0, query_width),
        qkv_part(query_width, query_width + HD),
        qkv_part(query_width + HD, query_width + 2 * HD),
        finish_cols(out_tile),
        finish_rows(gate_tile)(0, ff_width),
        finish_rows(up_tile)(0, ff_width),
        finish_cols(down_tile),
        gain_out[0],
        gain_out[1],
    )


def solution(mesh):
    placed = (
        P(("dp", "col"), "row"),
        P("row"),
        P("row", "col"),
        P("row", "col"),
        P("row", "col"),
        P("col", "row"),
        P("row"),
        P("row", "col"),
        P("row", "col"),
        P("col", "row"),
        P("dp", None),
        P(("dp", "col"), "row"),
    )
    return jax.shard_map(
        shards,
        mesh=mesh,
        in_specs=placed,
        out_specs=(
            P(("dp", "col"), "row"),
            P(("dp", "col"), "row"),
            P(("row", "dp"), "col"),
            P(("row", "dp"), "col"),
            P(("row", "dp"), "col"),
            P(("col", "dp"), "row"),
            P(("row", "dp"), "col"),
            P(("row", "dp"), "col"),
            P(("col", "dp"), "row"),
            P(("row", "dp")),
            P(("row", "dp")),
        ),
        check_vma=False,
    )
```

time: 2350 us -> 1250 us (0.53)
  waiting for transfers between devices: 1840 us -> 552 us
  starting transfers between devices: 2.51 us -> 99.1 us
  local copies, waits for them, and re-layouts: 30.9 us -> 114 us
    reduce_scatter x17 -> x5, waiting for transfers between devices: 1010 us -> 0.01 us  [weight_grad(): lax.psum_scatter(kept.astype(BF), 'row', scatter_dimension=0, tiled=True)]
    all_gather x8 -> x5, waiting for transfers between devices: 827 us -> 0.02 us  [fetch(): own = lax.all_gather(piece, 'row', axis=0, tiled=True)]
    ppermute x0 -> x44, waiting for transfers between devices: none -> 509 us  [the longest x10 348 us: from_y(): return lax.ppermute(v, 'dp', swap_y)]
    ppermute x0 -> x44, starting transfers between devices: none -> 54.4 us  [the longest x10 14.6 us: from_y(): return lax.ppermute(v, 'dp', swap_y)]
    all_to_all x0 -> x4, starting transfers between devices: none -> 44.4 us  [the longest x2 24.8 us: to_tokens(): came = lax.all_to_all(sent, 'row', split_axis=0, concat_axis=0, tiled=True)]
    all_to_all x0 -> x4, waiting for transfers between devices: none -> 42.7 us  [the longest x2 42.7 us: to_tokens(): came = lax.all_to_all(sent, 'row', split_axis=0, concat_axis=0, tiled=True)]
    psum x5 -> x1, blocking collectives: 53.2 us -> 13.3 us  [shards(): lax.psum(gain_rows, ('dp', 'col')).reshape(2, dp_size, feat // dp_size)]
    unnamed x1, blocking collectives: 6.04 us -> 40.6 us
  transfers between devices with their start and end apart: 25 -> 58, of which waited for: 24 -> 21; matrix products, arithmetic and copies ran while one was open for 8% -> 33% of each run, Pallas kernels for 0% -> 0%
where the time goes in v1:
time: 1250 us; the launch traced here: 1240 us
  waiting for transfers between devices  552 us (44%)
  matrix products  279 us (22%)
  local copies, waits for them, and re-layouts  114 us (9%)
  starting transfers between devices  99.1 us (8%)
  other arithmetic  93.1 us (7%)
  blocking collectives  90.7 us (7%)
  between operations  16.3 us (1%)
    ppermute x10, waiting for transfers between devices, from_y(): return lax.ppermute(v, 'dp', swap_y)  348 us
    dot_general x30, matrix products, contract(): lax.dot_general(left_side, right_side, (((left_dim,), (right_dim,)), ((),...  135 us
    ppermute x8, waiting for transfers between devices, from_x(): return lax.ppermute(v, 'col', [(0, 1), (1, 0)])  115 us
    all_to_all x2, waiting for transfers between devices, to_tokens(): came = lax.all_to_all(sent, 'row', split_axis=0, concat_axis=0, tiled=True)  42.7 us
    unnamed x1, blocking collectives  40.6 us
    dot_general x1, matrix products, shards(): jnp.einsum('bqhd,bkd->bqhk', grad_attended, values_all, preferred_element...  37 us
    all_gather x1, blocking collectives, shards(): lax.all_gather(y_order(jnp.stack([gain_attn, gain_mlp])).reshape(2, 2, ha...  36.7 us
    ppermute x3, waiting for transfers between devices, shards(): lax.ppermute(kv_here, 'row', row_shift(j)).reshape(2, per_seq, 2 * HD)  26.5 us
  transfers between devices with their start and end apart: 58, of which 21 were waited for; matrix products, arithmetic and copies ran while one was open for 33% of the time, Pallas kernels for 0%

profile of v1, /device:TPU:0, one launch (start us, length us, event | category | flops | bytes accessed | tf_op | source)
XLA Modules:
  0.0 1243.9 jit_solution(581878880018664143)
XLA Ops:
  25.7 6.3 all-to-all-start
  38.9 36.7 %all_gather.18 = bf16[2,2,4,256]{3,1,0,2:T(2,128)(2,1)S(1)} all-gather(bf16[2,2,1,256]{3,1,0,2:T(2,128)(2,1)S(1)} %copy.305), channel_id=1, replica_groups=mesh['dp'=4,'row'=4,'col'=2] {'row'}, dimensions={2}, use_global_device_ids=true | all-gather | bytes 10240 | tf_op jit(solution)/shard_map/all_gather | solution.py:268
  86.5 18.3 %collective-permute-done.1 = bf16[256,2048]{0,1:T(8,128)(2,1)} collective-permute-done((bf16[256,2048]{0,1:T(8,128)(2,1)}, bf16[256,2048]{0,1:T(8,128)(2,1)}, u32[]{:S(2)}, u32[]{:S(2)}) %collective-permute-start.1) | collective-permute-done | bytes 1048608 | tf_op jit(solution)/shard_map/ppermute | solution.py:109
  114.7 22.2 %collective-permute-done.4 = bf16[1024,640]{1,0:T(8,128)(2,1)} collective-permute-done((bf16[1024,640]{1,0:T(8,128)(2,1)}, bf16[1024,640]{1,0:T(8,128)(2,1)}, u32[]{:S(2)}, u32[]{:S(2)}) %collective-permute-start.4) | collective-permute-done | bytes 1310752 | tf_op jit(solution)/shard_map/ppermute | solution.py:106
  142.2 10.8 collective-permute-start.7
  159.1 5.1 collective-permute-done.7
  165.4 21.3 %collective-permute-done.6 = bf16[1024,128]{0,1:T(8,128)(2,1)} collective-permute-done((bf16[1024,128]{0,1:T(8,128)(2,1)S(1)}, bf16[1024,128]{0,1:T(8,128)(2,1)}, u32[]{:S(2)}, u32[]{:S(2)}) %collective-permute-start.6) | collective-permute-done | bytes 262176 | tf_op jit(solution)/shard_map/ppermute | solution.py:300
  195.4 25.9 %fusion.125 = (f32[2,512,8]{1,2,0:T(8,128)S(1)}, f32[2,512,8,2048]{3,1,2,0:T(8,128)}) fusion(bf16[2,512,8,64]{1,3,2,0:T(8,128)(2,1)} %bitcast_dynamic-update-slice_fusion, bf16[2,2048,128]{1,2,0:T(8,128)(2,1)} %reshape.757, pred[2,512,2048]{2,1,0:T(8,128)(4,1)} %compare_and_fusion), kind=kOutput, calls=%fused_computation.305 | convolution fusion | flops 2197807104 | bytes 70811648 | tf_op jit(solution)/shard_map/bqhd,bkd->bqhk/dot_general | solution.py:314
  221.3 21.5 %fusion = f32[2,512,8]{1,2,0:T(8,128)S(1)} fusion(f32[2,512,8,2048]{3,1,2,0:T(8,128)} %get-tuple-element.143, f32[2,512,8]{1,2,0:T(8,128)S(1)} %get-tuple-element.142, pred[2,512,2048]{2,1,0:T(8,128)(4,1)S(1)} %copy-done.15), kind=kLoop, calls=%fused_computation.9 | loop fusion | flops 50323456 | bytes 69271552 | tf_op jit(solution)/shard_map/reduce_sum | solution.py:322
  242.8 25.6 %fusion.126 = (bf16[2,512,8,64]{1,3,2,0:T(8,128)(2,1)}, f32[2,512,8,64]{1,3,2,0:T(8,128)}) fusion(f32[2,512,8]{1,2,0:T(8,128)S(1)} %fusion, bf16[2,2048,128]{1,2,0:T(8,128)(2,1)} %reshape.757, f32[2,512,8,2048]{3,1,2,0:T(8,128)} %get-tuple-element.143, f32[2,512,8]{1,2,0:T(8,128)S(1)} %get-tuple-element.142, pred[2,512,2048]{2,1,0:T(8,128)(4,1)} %compare_and_fusion), kind=kOutput, calls=%fused_computation.306 | convolution fusion | flops 2198863872 | bytes 72941568 | tf_op jit(solution)/shard_map/bqhk,bkd->bqhd/dot_general | solution.py:324
  283.5 18.4 %all-to-all-start.2 = ((bf16[4,256,512]{2,1,0:T(8,128)(2,1)}), bf16[4,256,512]{2,1,0:T(8,128)(2,1)}, u32[]{:S(2)}, u32[]{:S(2)}) async-start(bf16[4,256,512]{2,1,0:T(8,128)(2,1)} %bitcast.345), calls=%async_computation.2 | async-start | bytes 2097152 | tf_op jit(solution)/shard_map/all_to_all | solution.py:139
  306.6 42.7 %all-to-all-done.2 = bf16[4,256,512]{2,1,0:T(8,128)(2,1)} async-done(((bf16[4,256,512]{2,1,0:T(8,128)(2,1)}), bf16[4,256,512]{2,1,0:T(8,128)(2,1)}, u32[]{:S(2)}, u32[]{:S(2)}) %all-to-all-start.2) | async-done | bytes 1048608 | tf_op jit(solution)/shard_map/all_to_all | solution.py:139
  364.7 15.9 %collective-permute-done.19 = bf16[256,2048]{0,1:T(8,128)(2,1)} collective-permute-done((bf16[256,2048]{0,1:T(8,128)(2,1)}, bf16[256,2048]{0,1:T(8,128)(2,1)}, u32[]{:S(2)}, u32[]{:S(2)}) %collective-permute-start.19) | collective-permute-done | bytes 1048608 | tf_op jit(solution)/shard_map/ppermute | solution.py:109
  386.9 5.3 collective-permute-done.10
  404.1 12.2 collective-permute-done.11
  418.8 9.8 collective-permute-done.16
  428.6 7.1 fusion.40
  436.3 54.1 %collective-permute-done.14 = bf16[1024,1408]{1,0:T(8,128)(2,1)} collective-permute-done((bf16[1024,1408]{1,0:T(8,128)(2,1)}, bf16[1024,1408]{1,0:T(8,128)(2,1)}, u32[]{:S(2)}, u32[]{:S(2)}) %collective-permute-start.14) | collective-permute-done | bytes 2883616 | tf_op jit(solution)/shard_map/ppermute | solution.py:106
  490.4 5.4 fusion.71
  495.8 5.5 convolution_add_fusion.2
  501.3 39.3 %collective-permute-done.15 = bf16[1024,1408]{1,0:T(8,128)(2,1)S(1)} collective-permute-done((bf16[1024,1408]{1,0:T(8,128)(2,1)}, bf16[1024,1408]{1,0:T(8,128)(2,1)S(1)}, u32[]{:S(2)}, u32[]{:S(2)}) %collective-permute-start.15) | collective-permute-done | bytes 2883616 | tf_op jit(solution)/shard_map/ppermute | solution.py:106
  545.8 5.4 convolution_add_fusion.1
  551.2 11.8 multiply_convert_fusion.1
  563.0 6.3 fusion.129
  569.3 5.0 fusion.21
  574.3 5.3 fusion.130
  579.7 5.0 fusion.18
  584.7 5.8 maximum_add_fusion
  595.8 5.3 fusion.128
  608.4 20.1 %collective-permute-done.23 = bf16[256,2048]{0,1:T(8,128)(2,1)S(1)} collective-permute-done((bf16[256,2048]{0,1:T(8,128)(2,1)S(1)}, bf16[256,2048]{0,1:T(8,128)(2,1)S(1)}, u32[]{:S(2)}, u32[]{:S(2)}) %collective-permute-start.23) | collective-permute-done | bytes 1048608 | tf_op jit(solution)/shard_map/ppermute | solution.py:109
  629.9 20.5 %collective-permute-done.18 = bf16[256,2048]{0,1:T(8,128)(2,1)S(1)} collective-permute-done((bf16[256,2048]{0,1:T(8,128)(2,1)S(1)}, bf16[256,2048]{0,1:T(8,128)(2,1)S(1)}, u32[]{:S(2)}, u32[]{:S(2)}) %collective-permute-start.18) | collective-permute-done | bytes 1048608 | tf_op jit(solution)/shard_map/ppermute | solution.py:109
  655.4 23.0 %collective-permute-done.24 = bf16[256,2048]{0,1:T(8,128)(2,1)S(1)} collective-permute-done((bf16[256,2048]{0,1:T(8,128)(2,1)S(1)}, bf16[256,2048]{0,1:T(8,128)(2,1)S(1)}, u32[]{:S(2)}, u32[]{:S(2)}) %collective-permute-start.24) | collective-permute-done | bytes 1048608 | tf_op jit(solution)/shard_map/ppermute | solution.py:109
  678.4 4.9 convolution_convert_fusion.2
  687.6 83.2 %collective-permute-done.34 = bf16[1024,512]{1,0:T(8,128)(2,1)S(1)} collective-permute-done((bf16[1024,512]{1,0:T(8,128)(2,1)S(1)}, bf16[1024,512]{1,0:T(8,128)(2,1)S(1)}, u32[]{:S(2)}, u32[]{:S(2)}) %collective-permute-start.34) | collective-permute-done | bytes 1048608 | tf_op jit(solution)/shard_map/ppermute | solution.py:106
  773.2 8.4 add_convert_fusion.2
  783.4 5.4 convolution_convert_fusion.1
  790.6 62.3 %collective-permute-done.39 = bf16[1024,1408]{1,0:T(8,128)(2,1)S(1)} collective-permute-done((bf16[1024,1408]{1,0:T(8,128)(2,1)S(1)}, bf16[1024,1408]{1,0:T(8,128)(2,1)S(1)}, u32[]{:S(2)}, u32[]{:S(2)}) %collective-permute-start.39) | collective-permute-done | bytes 2883616 | tf_op jit(solution)/shard_map/ppermute | solution.py:106
  857.8 6.0 convolution_convert_fusion
  865.7 61.6 %collective-permute-done.41 = bf16[1024,1408]{1,0:T(8,128)(2,1)S(1)} collective-permute-done((bf16[1024,1408]{1,0:T(8,128)(2,1)S(1)}, bf16[1024,1408]{1,0:T(8,128)(2,1)S(1)}, u32[]{:S(2)}, u32[]{:S(2)}) %collective-permute-start.41) | collective-permute-done | bytes 2883616 | tf_op jit(solution)/shard_map/ppermute | solution.py:106
  934.3 15.8 %all-to-all-start.1 = ((bf16[4,256,512]{1,2,0:T(8,128)(2,1)}), bf16[4,256,512]{1,2,0:T(8,128)(2,1)}, u32[]{:S(2)}, u32[]{:S(2)}) async-start(bf16[4,256,512]{1,2,0:T(8,128)(2,1)} %bitcast.67), calls=%async_computation.1 | async-start | bytes 2097152 | tf_op jit(solution)/shard_map/all_to_all | solution.py:146
  963.7 25.0 %fusion.24 = f32[2,2048,64]{1,2,0:T(8,128)} fusion(bf16[2,512,8,64]{1,3,2,0:T(8,128)(2,1)} %copy.339, f32[2,512,8,2048]{3,1,2,0:T(8,128)} %get-tuple-element.143, f32[2,512,8]{1,2,0:T(8,128)S(1)} %log_add_fusion, pred[2,512,2048]{2,1,0:T(8,128)(4,1)S(1)} %copy-done.16), kind=kOutput, calls=%fused_computation.62 | convolution fusion | flops 2197815296 | bytes 71335936 | tf_op jit(solution)/shard_map/bqhk,bqhd->bkd/dot_general | solution.py:369
  990.9 37.0 %multiply_convert_fusion = bf16[2,512,8,2048]{3,1,2,0:T(8,128)(2,1)} fusion(f32[2,512,8,2048]{3,1,2,0:T(8,128)} %get-tuple-element.143, bf16[2,512,8,64]{1,3,2,0:T(8,128)(2,1)S(1)} %copy-done.20, f32[2,512,8]{1,2,0:T(8,128)S(1)} %multiply_reduce_fusion.3, f32[2,512,8]{1,2,0:T(8,128)S(1)} %log_add_fusion, pred[2,512,2048]{2,1,0:T(8,128)(4,1)S(1)} %copy-done.16, ...), kind=kOutput, calls=%fused_computation.5 | convolution fusion | flops 2231369728 | bytes 104398848 | tf_op jit(solution)/shard_map/bqhd,bkd->bqhk/dot_general | solution.py:359
  1027.9 13.8 %fusion.27 = f32[2,2048,64]{1,2,0:T(8,128)S(1)} fusion(bf16[2,512,8,64]{1,3,2,0:T(8,128)(2,1)S(1)} %copy-done.19, bf16[2,512,8,2048]{3,1,2,0:T(8,128)(2,1)} %multiply_convert_fusion), kind=kOutput, calls=%fused_computation.64 | convolution fusion | flops 2147745792 | bytes 35651584 | tf_op jit(solution)/shard_map/bqhk,bqhd->bkd/dot_general | solution.py:366
  1041.7 16.3 %multiply_bitcast_fusion = f32[2,8,8,8,512]{4,3,2,1,0:T(8,128)} fusion(bf16[2,512,8,2048]{3,1,2,0:T(8,128)(2,1)} %multiply_convert_fusion, bf16[2,2048,128]{1,2,0:T(8,128)(2,1)S(1)} %copy-done.33), kind=kOutput, calls=%fused_computation.83 | convolution fusion | flops 2148007936 | bytes 36175872 | tf_op jit(solution)/shard_map/bqhk,bkd->bqhd/dot_general | solution.py:363
  1076.5 14.0 %collective-permute-done.28 = bf16[1024,128]{0,1:T(8,128)(2,1)S(1)} collective-permute-done((bf16[1024,128]{0,1:T(8,128)(2,1)S(1)}, bf16[1024,128]{0,1:T(8,128)(2,1)S(1)}, u32[]{:S(2)}, u32[]{:S(2)}) %collective-permute-start.28) | collective-permute-done | bytes 262176 | tf_op jit(solution)/shard_map/ppermute | solution.py:376
  1123.7 15.3 %collective-permute-done.32 = bf16[1024,640]{1,0:T(8,128)(2,1)} collective-permute-done((bf16[1024,640]{1,0:T(8,128)(2,1)}, bf16[1024,640]{1,0:T(8,128)(2,1)}, u32[]{:S(2)}, u32[]{:S(2)}) %collective-permute-start.32) | collective-permute-done | bytes 1310752 | tf_op jit(solution)/shard_map/ppermute | solution.py:106
  1165.0 40.6 %all-reduce.1 = f32[4,2,2,256]{3,2,1,0:T(2,128)S(1)} all-reduce(f32[4,2,2,256]{3,2,1,0:T(2,128)S(1)} %copy.354), channel_id=11, replica_groups=mesh['dp'=4,'row'=4,'col'=2] {'row'}, use_global_device_ids=true, to_apply=%region_16.17.clone | all-reduce | flops 4096 | bytes 32768
  1206.4 13.3 %psum.7 = f32[2,4,128]{2,1,0:T(4,128)S(1)} all-reduce(f32[2,4,128]{2,1,0:T(4,128)S(1)} %reshape.798), channel_id=1, replica_groups=mesh['dp'=4,'row'=4,'col'=2] {'dp','col'}, use_global_device_ids=true, to_apply=%region_17.18 | all-reduce | flops 1024 | bytes 8192 | tf_op jit(solution)/shard_map/psum | solution.py:393
  (493 shorter events, 281.6 us)
Async XLA Ops:
  7.2 97.6 %all-gather.10.cloned.1.call-start = ((), (), s32[]{:S(2)}) async-start(), calls=%async_computation.9 | async-start | bytes 1638400 | tf_op jit(solution)/shard_map/all_gather | solution.py:167
  12.9 98.9 %all-gather.12.cloned.1.call-start = ((), (), s32[]{:S(2)}) async-start(), calls=%async_computation.15 | async-start | bytes 1310720 | tf_op jit(solution)/shard_map/all_gather | solution.py:167
  16.7 346.2 %all-gather.18.cloned.1.call-start = ((), (), s32[]{:S(2)}) async-start(), calls=%async_computation.18 | async-start | bytes 3604480 | tf_op jit(solution)/shard_map/all_gather | solution.py:167
  25.7 50.7 %all-to-all-start = ((bf16[4,256,512]{2,1,0:T(8,128)(2,1)}), bf16[4,256,512]{2,1,0:T(8,128)(2,1)S(1)}, u32[]{:S(2)}, u32[]{:S(2)}) async-start(bf16[4,256,512]{2,1,0:T(8,128)(2,1)} %bitcast.6), calls=%async_computation | async-start | bytes 2097152 | tf_op jit(solution)/shard_map/all_to_all | solution.py:139
  32.0 348.6 %all-gather.14.cloned.1.call-start = ((), (), s32[]{:S(2)}) async-start(), calls=%async_computation.16 | async-start | bytes 3604480 | tf_op jit(solution)/shard_map/all_gather | solution.py:167
  32.0 52.5 %collective-permute-start = (s32[1,2048]{1,0:T(1,128)S(1)}, s32[1,2048]{1,0:T(1,128)S(1)}, u32[]{:S(2)}, u32[]{:S(2)}) collective-permute-start(s32[1,2048]{1,0:T(1,128)S(1)} %copy-done.56), channel_id=1, source_target_pairs={{0,8},{8,0},{16,24},{24,16},{1,9},{9,1},{17,25},{25,17},{2,10},{10... | collective-permute-start | bytes 24584 | tf_op jit(solution)/shard_map/ppermute | solution.py:103
  81.6 23.2 %collective-permute-start.1 = (bf16[256,2048]{0,1:T(8,128)(2,1)}, bf16[256,2048]{0,1:T(8,128)(2,1)}, u32[]{:S(2)}, u32[]{:S(2)}) collective-permute-start(bf16[256,2048]{0,1:T(8,128)(2,1)} %multiply_convert_fusion.5), channel_id=1, source_target_pairs={{0,1},{1,0},{2,3},{3,2},{4,5},{5,4},{6,7},{7,6},{8,9},{9,8},{10,11... | collective-permute-start | bytes 3145736 | tf_op jit(solution)/shard_map/ppermute | solution.py:109
  86.4 25.8 %collective-permute-start.2 = (bf16[256,2048]{0,1:T(8,128)(2,1)}, bf16[256,2048]{0,1:T(8,128)(2,1)}, u32[]{:S(2)}, u32[]{:S(2)}) collective-permute-start(bf16[256,2048]{0,1:T(8,128)(2,1)} %multiply_convert_fusion.5), channel_id=1, source_target_pairs={{0,8},{8,0},{16,24},{24,16},{1,9},{9,1},{17,25},{25,17},{2,10},{10... | collective-permute-start | bytes 3145736 | tf_op jit(solution)/shard_map/ppermute | solution.py:103
  104.8 32.0 %collective-permute-start.4 = (bf16[1024,640]{1,0:T(8,128)(2,1)}, bf16[1024,640]{1,0:T(8,128)(2,1)}, u32[]{:S(2)}, u32[]{:S(2)}) collective-permute-start(bf16[1024,640]{1,0:T(8,128)(2,1)} %all-gather.10.cloned.1.call-done), channel_id=1, source_target_pairs={{0,16},{8,24},{16,0},{24,8},{1,17},{9,25},{17,1},{25,9},{2,18},{10... | collective-permute-start | bytes 3932168 | tf_op jit(solution)/shard_map/ppermute | solution.py:106
  111.7 160.5 %collective-permute-start.8 = (bf16[1024,512]{1,0:T(8,128)(2,1)}, bf16[1024,512]{1,0:T(8,128)(2,1)}, u32[]{:S(2)}, u32[]{:S(2)}) collective-permute-start(bf16[1024,512]{1,0:T(8,128)(2,1)} %bitcast.420), channel_id=1, source_target_pairs={{0,16},{8,24},{16,0},{24,8},{1,17},{9,25},{17,1},{25,9},{2,18},{10... | collective-permute-start | bytes 3145736 | tf_op jit(solution)/shard_map/ppermute | solution.py:106
  142.2 22.0 %collective-permute-start.7 = (bf16[1024,128]{0,1:T(8,128)(2,1)S(1)}, bf16[1024,128]{0,1:T(8,128)(2,1)}, u32[]{:S(2)}, u32[]{:S(2)}) collective-permute-start(bf16[1024,128]{0,1:T(8,128)(2,1)S(1)} %pad_maximum_fusion.20), channel_id=1, source_target_pairs={{0,2},{2,4},{4,6},{6,0},{1,3},{3,5},{5,7},{7,1},{8,10},{10,12},{12... | collective-permute-start | bytes 786440 | tf_op jit(solution)/shard_map/ppermute | solution.py:300
  153.0 33.6 %collective-permute-start.6 = (bf16[1024,128]{0,1:T(8,128)(2,1)S(1)}, bf16[1024,128]{0,1:T(8,128)(2,1)}, u32[]{:S(2)}, u32[]{:S(2)}) collective-permute-start(bf16[1024,128]{0,1:T(8,128)(2,1)S(1)} %pad_maximum_fusion.20), channel_id=1, source_target_pairs={{0,4},{2,6},{4,0},{6,2},{1,5},{3,7},{5,1},{7,3},{8,12},{10,14},{12... | collective-permute-start | bytes 786440 | tf_op jit(solution)/shard_map/ppermute | solution.py:300
  154.7 33.1 %collective-permute-start.5 = (bf16[1024,128]{0,1:T(8,128)(2,1)S(1)}, bf16[1024,128]{0,1:T(8,128)(2,1)}, u32[]{:S(2)}, u32[]{:S(2)}) collective-permute-start(bf16[1024,128]{0,1:T(8,128)(2,1)S(1)} %pad_maximum_fusion.20), channel_id=1, source_target_pairs={{0,6},{2,0},{4,2},{6,4},{1,7},{3,1},{5,3},{7,5},{8,14},{10,8},{12,... | collective-permute-start | bytes 786440 | tf_op jit(solution)/shard_map/ppermute | solution.py:300
  278.2 77.7 %collective-permute-start.9 = (bf16[512,2048]{0,1:T(8,128)(2,1)}, bf16[512,2048]{0,1:T(8,128)(2,1)}, u32[]{:S(2)}, u32[]{:S(2)}) collective-permute-start(bf16[512,2048]{0,1:T(8,128)(2,1)} %fusion.17), channel_id=1, source_target_pairs={{0,8},{8,0},{16,24},{24,16},{1,9},{9,1},{17,25},{25,17},{2,10},{10... | collective-permute-start | bytes 6291464 | tf_op jit(solution)/shard_map/ppermute | solution.py:103
  283.5 65.8 %all-to-all-start.2 = ((bf16[4,256,512]{2,1,0:T(8,128)(2,1)}), bf16[4,256,512]{2,1,0:T(8,128)(2,1)}, u32[]{:S(2)}, u32[]{:S(2)}) async-start(bf16[4,256,512]{2,1,0:T(8,128)(2,1)} %bitcast.345), calls=%async_computation.2 | async-start | bytes 2097152 | tf_op jit(solution)/shard_map/all_to_all | solution.py:139
  301.9 96.1 %all-gather.16.cloned.1.call-start = ((), (), s32[]{:S(2)}) async-start(), calls=%async_computation.17 | async-start | bytes 3604480 | tf_op jit(solution)/shard_map/all_gather | solution.py:167
  306.5 812.7 %reduce-scatter.8.cloned.1.call-start = ((), (), s32[]{:S(2)}) async-start(), calls=%async_computation.11 | async-start | bytes 1310720 | tf_op jit(solution)/shard_map/reduce_scatter | solution.py:183
  354.2 26.3 %collective-permute-start.19 = (bf16[256,2048]{0,1:T(8,128)(2,1)}, bf16[256,2048]{0,1:T(8,128)(2,1)}, u32[]{:S(2)}, u32[]{:S(2)}) collective-permute-start(bf16[256,2048]{0,1:T(8,128)(2,1)} %bitcast.84), channel_id=1, source_target_pairs={{0,1},{1,0},{2,3},{3,2},{4,5},{5,4},{6,7},{7,6},{8,9},{9,8},{10,11... | collective-permute-start | bytes 3145736 | tf_op jit(solution)/shard_map/ppermute | solution.py:109
  362.5 29.7 %collective-permute-start.10 = (bf16[256,2048]{0,1:T(8,128)(2,1)}, bf16[256,2048]{0,1:T(8,128)(2,1)}, u32[]{:S(2)}, u32[]{:S(2)}) collective-permute-start(bf16[256,2048]{0,1:T(8,128)(2,1)} %slice.613), channel_id=1, source_target_pairs={{0,1},{1,0},{2,3},{3,2},{4,5},{5,4},{6,7},{7,6},{8,9},{9,8},{10,11... | collective-permute-start | bytes 3145736 | tf_op jit(solution)/shard_map/ppermute | solution.py:109
  362.9 65.7 %collective-permute-start.16 = (bf16[1024,1408]{1,0:T(8,128)(2,1)}, bf16[1024,1408]{1,0:T(8,128)(2,1)}, u32[]{:S(2)}, u32[]{:S(2)}) collective-permute-start(bf16[1024,1408]{1,0:T(8,128)(2,1)} %bitcast.419), channel_id=1, source_target_pairs={{0,16},{8,24},{16,0},{24,8},{1,17},{9,25},{17,1},{25,9},{2,18},{10... | collective-permute-start | bytes 8650760 | tf_op jit(solution)/shard_map/ppermute | solution.py:106
  364.6 38.0 %collective-permute-start.20 = (bf16[256,2048]{0,1:T(8,128)(2,1)}, bf16[256,2048]{0,1:T(8,128)(2,1)}, u32[]{:S(2)}, u32[]{:S(2)}) collective-permute-start(bf16[256,2048]{0,1:T(8,128)(2,1)} %bitcast.84), channel_id=1, source_target_pairs={{0,8},{8,0},{16,24},{24,16},{1,9},{9,1},{17,25},{25,17},{2,10},{10... | collective-permute-start | bytes 3145736 | tf_op jit(solution)/shard_map/ppermute | solution.py:103
  380.6 23.5 %collective-permute-start.21 = (bf16[256,2048]{0,1:T(8,128)(2,1)}, bf16[256,2048]{0,1:T(8,128)(2,1)}, u32[]{:S(2)}, u32[]{:S(2)}) collective-permute-start(bf16[256,2048]{0,1:T(8,128)(2,1)} %collective-permute-done.19), channel_id=1, source_target_pairs={{0,8},{8,0},{16,24},{24,16},{1,9},{9,1},{17,25},{25,17},{2,10},{10... | collective-permute-start | bytes 3145736 | tf_op jit(solution)/shard_map/ppermute | solution.py:103
  385.1 105.2 %collective-permute-start.14 = (bf16[1024,1408]{1,0:T(8,128)(2,1)}, bf16[1024,1408]{1,0:T(8,128)(2,1)}, u32[]{:S(2)}, u32[]{:S(2)}) collective-permute-start(bf16[1024,1408]{1,0:T(8,128)(2,1)} %bitcast.357), channel_id=1, source_target_pairs={{0,16},{8,24},{16,0},{24,8},{1,17},{9,25},{17,1},{25,9},{2,18},{10... | collective-permute-start | bytes 8650760 | tf_op jit(solution)/shard_map/ppermute | solution.py:106
  402.6 138.0 %collective-permute-start.15 = (bf16[1024,1408]{1,0:T(8,128)(2,1)}, bf16[1024,1408]{1,0:T(8,128)(2,1)S(1)}, u32[]{:S(2)}, u32[]{:S(2)}) collective-permute-start(bf16[1024,1408]{1,0:T(8,128)(2,1)} %bitcast.358), channel_id=1, source_target_pairs={{0,16},{8,24},{16,0},{24,8},{1,17},{9,25},{17,1},{25,9},{2,18},{10... | collective-permute-start | bytes 8650760 | tf_op jit(solution)/shard_map/ppermute | solution.py:106
  404.1 31.5 %collective-permute-start.12 = (bf16[256,2048]{0,1:T(8,128)(2,1)S(1)}, bf16[256,2048]{0,1:T(8,128)(2,1)S(1)}, u32[]{:S(2)}, u32[]{:S(2)}) collective-permute-start(bf16[256,2048]{0,1:T(8,128)(2,1)S(1)} %multiply_convert_fusion.4), channel_id=1, source_target_pairs={{0,8},{8,0},{16,24},{24,16},{1,9},{9,1},{17,25},{25,17},{2,10},{10... | collective-permute-start | bytes 3145736 | tf_op jit(solution)/shard_map/ppermute | solution.py:103
  602.4 26.1 %collective-permute-start.23 = (bf16[256,2048]{0,1:T(8,128)(2,1)S(1)}, bf16[256,2048]{0,1:T(8,128)(2,1)S(1)}, u32[]{:S(2)}, u32[]{:S(2)}) collective-permute-start(bf16[256,2048]{0,1:T(8,128)(2,1)S(1)} %slice.611), channel_id=1, source_target_pairs={{0,1},{1,0},{2,3},{3,2},{4,5},{5,4},{6,7},{7,6},{8,9},{9,8},{10,11... | collective-permute-start | bytes 3145736 | tf_op jit(solution)/shard_map/ppermute | solution.py:109
  606.6 43.8 %collective-permute-start.18 = (bf16[256,2048]{0,1:T(8,128)(2,1)S(1)}, bf16[256,2048]{0,1:T(8,128)(2,1)S(1)}, u32[]{:S(2)}, u32[]{:S(2)}) collective-permute-start(bf16[256,2048]{0,1:T(8,128)(2,1)S(1)} %slice.612), channel_id=1, source_target_pairs={{0,1},{1,0},{2,3},{3,2},{4,5},{5,4},{6,7},{7,6},{8,9},{9,8},{10,11... | collective-permute-start | bytes 3145736 | tf_op jit(solution)/shard_map/ppermute | solution.py:109
  653.7 24.7 %collective-permute-start.24 = (bf16[256,2048]{0,1:T(8,128)(2,1)S(1)}, bf16[256,2048]{0,1:T(8,128)(2,1)S(1)}, u32[]{:S(2)}, u32[]{:S(2)}) collective-permute-start(bf16[256,2048]{0,1:T(8,128)(2,1)S(1)} %get-tuple-element.70), channel_id=1, source_target_pairs={{0,1},{1,0},{2,3},{3,2},{4,5},{5,4},{6,7},{7,6},{8,9},{9,8},{10,11... | collective-permute-start | bytes 3145736 | tf_op jit(solution)/shard_map/ppermute | solution.py:109
  655.4 29.7 %collective-permute-start.25 = (bf16[256,2048]{0,1:T(8,128)(2,1)S(1)}, bf16[256,2048]{0,1:T(8,128)(2,1)S(1)}, u32[]{:S(2)}, u32[]{:S(2)}) collective-permute-start(bf16[256,2048]{0,1:T(8,128)(2,1)S(1)} %get-tuple-element.70), channel_id=1, source_target_pairs={{0,8},{8,0},{16,24},{24,16},{1,9},{9,1},{17,25},{25,17},{2,10},{10... | collective-permute-start | bytes 3145736 | tf_op jit(solution)/shard_map/ppermute | solution.py:103
  683.3 89.9 %collective-permute-start.37 = (bf16[1024,1408]{1,0:T(8,128)(2,1)}, bf16[1024,1408]{1,0:T(8,128)(2,1)}, u32[]{:S(2)}, u32[]{:S(2)}) collective-permute-start(bf16[1024,1408]{1,0:T(8,128)(2,1)} %convolution_convert_fusion.2), channel_id=1, source_target_pairs={{0,16},{8,24},{16,0},{24,8},{1,17},{9,25},{17,1},{25,9},{2,18},{10... | collective-permute-start | bytes 8650760 | tf_op jit(solution)/shard_map/ppermute | solution.py:106
  687.0 83.9 %collective-permute-start.34 = (bf16[1024,512]{1,0:T(8,128)(2,1)S(1)}, bf16[1024,512]{1,0:T(8,128)(2,1)S(1)}, u32[]{:S(2)}, u32[]{:S(2)}) collective-permute-start(bf16[1024,512]{1,0:T(8,128)(2,1)S(1)} %fusion.58), channel_id=1, source_target_pairs={{0,16},{8,24},{16,0},{24,8},{1,17},{9,25},{17,1},{25,9},{2,18},{10... | collective-permute-start | bytes 3145736 | tf_op jit(solution)/shard_map/ppermute | solution.py:106
  773.2 371.6 %reduce-scatter.10.cloned.1.call-start = ((), (), s32[]{:S(2)}) async-start(), calls=%async_computation.12 | async-start | bytes 3604480 | tf_op jit(solution)/shard_map/reduce_scatter | solution.py:183
  781.6 364.9 %reduce-scatter.12.cloned.1.call-start = ((), (), s32[]{:S(2)}) async-start(), calls=%async_computation.13 | async-start | bytes 3604480 | tf_op jit(solution)/shard_map/reduce_scatter | solution.py:183
  788.8 64.1 %collective-permute-start.39 = (bf16[1024,1408]{1,0:T(8,128)(2,1)S(1)}, bf16[1024,1408]{1,0:T(8,128)(2,1)S(1)}, u32[]{:S(2)}, u32[]{:S(2)}) collective-permute-start(bf16[1024,1408]{1,0:T(8,128)(2,1)S(1)} %convolution_convert_fusion.1), channel_id=1, source_target_pairs={{0,16},{8,24},{16,0},{24,8},{1,17},{9,25},{17,1},{25,9},{2,18},{10... | collective-permute-start | bytes 8650760 | tf_op jit(solution)/shard_map/ppermute | solution.py:106
  857.8 290.4 %reduce-scatter.14.cloned.1.call-start = ((), (), s32[]{:S(2)}) async-start(), calls=%async_computation.14 | async-start | bytes 3604480 | tf_op jit(solution)/shard_map/reduce_scatter | solution.py:183
  863.9 63.4 %collective-permute-start.41 = (bf16[1024,1408]{1,0:T(8,128)(2,1)S(1)}, bf16[1024,1408]{1,0:T(8,128)(2,1)S(1)}, u32[]{:S(2)}, u32[]{:S(2)}) collective-permute-start(bf16[1024,1408]{1,0:T(8,128)(2,1)S(1)} %convolution_convert_fusion), channel_id=1, source_target_pairs={{0,16},{8,24},{16,0},{24,8},{1,17},{9,25},{17,1},{25,9},{2,18},{10... | collective-permute-start | bytes 8650760 | tf_op jit(solution)/shard_map/ppermute | solution.py:106
  934.3 166.1 %all-to-all-start.1 = ((bf16[4,256,512]{1,2,0:T(8,128)(2,1)}), bf16[4,256,512]{1,2,0:T(8,128)(2,1)}, u32[]{:S(2)}, u32[]{:S(2)}) async-start(bf16[4,256,512]{1,2,0:T(8,128)(2,1)} %bitcast.67), calls=%async_computation.1 | async-start | bytes 2097152 | tf_op jit(solution)/shard_map/all_to_all | solution.py:146
  950.1 274.7 %reduce-scatter.6.cloned.1.call-start = ((), (), s32[]{:S(2)}) async-start(), calls=%async_computation.10 | async-start | bytes 1638400 | tf_op jit(solution)/shard_map/reduce_scatter | solution.py:183
  1069.9 20.6 %collective-permute-start.28 = (bf16[1024,128]{0,1:T(8,128)(2,1)S(1)}, bf16[1024,128]{0,1:T(8,128)(2,1)S(1)}, u32[]{:S(2)}, u32[]{:S(2)}) collective-permute-start(bf16[1024,128]{0,1:T(8,128)(2,1)S(1)} %bitcast.393), channel_id=1, source_target_pairs={{0,4},{2,6},{4,0},{6,2},{1,5},{3,7},{5,1},{7,3},{8,12},{10,14},{12... | collective-permute-start | bytes 786440 | tf_op jit(solution)/shard_map/ppermute | solution.py:376
  1107.5 31.5 %collective-permute-start.32 = (bf16[1024,640]{1,0:T(8,128)(2,1)}, bf16[1024,640]{1,0:T(8,128)(2,1)}, u32[]{:S(2)}, u32[]{:S(2)}) collective-permute-start(bf16[1024,640]{1,0:T(8,128)(2,1)} %fusion.55), channel_id=1, source_target_pairs={{0,16},{8,24},{16,0},{24,8},{1,17},{9,25},{17,1},{25,9},{2,18},{10... | collective-permute-start | bytes 3932168 | tf_op jit(solution)/shard_map/ppermute | solution.py:106
  1117.7 37.1 %collective-permute-start.31 = (bf16[256,2048]{0,1:T(8,128)(2,1)}, bf16[256,2048]{0,1:T(8,128)(2,1)}, u32[]{:S(2)}, u32[]{:S(2)}) collective-permute-start(bf16[256,2048]{0,1:T(8,128)(2,1)} %slice.610), channel_id=1, source_target_pairs={{0,1},{1,0},{2,3},{3,2},{4,5},{5,4},{6,7},{7,6},{8,9},{9,8},{10,11... | collective-permute-start | bytes 3145736 | tf_op jit(solution)/shard_map/ppermute | solution.py:109
  1121.0 22.9 %collective-permute-start.35 = (bf16[256,256]{1,0:T(8,128)(2,1)S(1)}, bf16[256,256]{1,0:T(8,128)(2,1)S(1)}, u32[]{:S(2)}, u32[]{:S(2)}) collective-permute-start(bf16[256,256]{1,0:T(8,128)(2,1)S(1)} %bitcast.402), channel_id=1, source_target_pairs={{0,0},{8,16},{16,8},{24,24},{1,1},{9,17},{17,9},{25,25},{2,2},{10,... | collective-permute-start | bytes 393224 | tf_op jit(solution)/shard_map/ppermute | solution.py:226
  1121.8 22.1 %collective-permute-start.36 = (bf16[256,256]{1,0:T(8,128)(2,1)S(1)}, bf16[256,256]{1,0:T(8,128)(2,1)S(1)}, u32[]{:S(2)}, u32[]{:S(2)}) collective-permute-start(bf16[256,256]{1,0:T(8,128)(2,1)S(1)} %bitcast.403), channel_id=1, source_target_pairs={{0,8},{8,24},{16,0},{24,16},{1,9},{9,25},{17,1},{25,17},{2,10},{10... | collective-permute-start | bytes 393224 | tf_op jit(solution)/shard_map/ppermute | solution.py:227
  1146.5 73.7 %collective-permute-start.38 = (bf16[128,1408]{1,0:T(8,128)(2,1)}, bf16[128,1408]{1,0:T(8,128)(2,1)}, u32[]{:S(2)}, u32[]{:S(2)}) collective-permute-start(bf16[128,1408]{1,0:T(8,128)(2,1)} %dynamic-slice_bitcast_fusion.3), channel_id=1, source_target_pairs={{0,8},{8,0},{16,24},{24,16},{1,9},{9,1},{17,25},{25,17},{2,10},{10... | collective-permute-start | bytes 1081352 | tf_op jit(solution)/shard_map/ppermute | solution.py:103
  1147.6 75.0 %collective-permute-start.40 = (bf16[128,1408]{1,0:T(8,128)(2,1)S(1)}, bf16[128,1408]{1,0:T(8,128)(2,1)}, u32[]{:S(2)}, u32[]{:S(2)}) collective-permute-start(bf16[128,1408]{1,0:T(8,128)(2,1)S(1)} %dynamic-slice_bitcast_fusion.2), channel_id=1, source_target_pairs={{0,8},{8,0},{16,24},{24,16},{1,9},{9,1},{17,25},{25,17},{2,10},{10... | collective-permute-start | bytes 1081352 | tf_op jit(solution)/shard_map/ppermute | solution.py:103
  1150.5 75.5 %collective-permute-start.42 = (bf16[704,256]{1,0:T(8,128)(2,1)}, bf16[704,256]{1,0:T(8,128)(2,1)S(1)}, u32[]{:S(2)}, u32[]{:S(2)}) collective-permute-start(bf16[704,256]{1,0:T(8,128)(2,1)} %get-tuple-element.111), channel_id=1, source_target_pairs={{0,0},{8,16},{16,8},{24,24},{1,1},{9,17},{17,9},{25,25},{2,2},{10,... | collective-permute-start | bytes 1081352 | tf_op jit(solution)/shard_map/ppermute | solution.py:226
  1152.7 73.3 %collective-permute-start.43 = (bf16[704,256]{1,0:T(8,128)(2,1)}, bf16[704,256]{1,0:T(8,128)(2,1)}, u32[]{:S(2)}, u32[]{:S(2)}) collective-permute-start(bf16[704,256]{1,0:T(8,128)(2,1)} %get-tuple-element.112), channel_id=1, source_target_pairs={{0,8},{8,24},{16,0},{24,16},{1,9},{9,25},{17,1},{25,17},{2,10},{10... | collective-permute-start | bytes 1081352 | tf_op jit(solution)/shard_map/ppermute | solution.py:227
  1161.2 69.7 %all-to-all-start.3 = ((bf16[4,256,512]{1,2,0:T(8,128)(2,1)}), bf16[4,256,512]{1,2,0:T(8,128)(2,1)S(1)}, u32[]{:S(2)}, u32[]{:S(2)}) async-start(bf16[4,256,512]{1,2,0:T(8,128)(2,1)} %bitcast.96), calls=%async_computation.3 | async-start | bytes 2097152 | tf_op jit(solution)/shard_map/all_to_all | solution.py:146
  (89 other events, 2083.2 us)
Sparse Core Ops, SparseCore 0:
  13.0 48.4 all-gather.9
  63.1 31.0 all-gather.11
  95.8 58.4 all-gather.17
  155.7 69.8 all-gather.13
  306.7 72.4 all-gather.15
  773.3 39.6 reduce-scatter.7
  815.3 54.8 reduce-scatter.9
  872.4 56.0 reduce-scatter.11
  932.2 85.0 reduce-scatter.13
  1144.0 38.8 reduce-scatter.5
